TPU v7x, 32 devices: a whole 2x2x4 slice. The times are simulated.
32 devices in a mesh: groups: 2 (over y), tm: 4 (over z), chan: 4 (over x, core).
Axes of the slice: x: 2, y: 2, z: 4, core: 2. Of those that a mesh axis runs over, the one named last changes fastest.
Arguments:
- vis: bfloat16 [8, 128, 2, 128], P(('groups', 'chan'), 'tm'), parts along dimension 0, may hold values from -6 to 6
- row_weight: bfloat16 [8, 128, 128, 128], P(('groups', 'chan'), 'tm'), parts along dimension 0, may hold values from -4 to 4
- col_weight: bfloat16 [8, 128, 128, 256], P(('groups', 'chan'), 'tm'), parts along dimension 0, may hold values from -0.5 to 0.5
- w_bin: int32 [8, 128, 1], P(('groups', 'chan'), 'tm'), parts along dimension 0, may hold values from 0 to 3; in each aligned block of 32 rows (0 to 31, 32 to 63, ..., all dimensions but the last counted through in order) at most 16 rows name the same one
- tile_col: int32 [8, 128], P(('groups', 'chan'), 'tm'), parts along dimension 0, may hold values from 0 to 15
- w_kernel: bfloat16 [8, 512, 512], P(('groups', 'tm')), parts along dimension 0, may hold values from -0.25 to 0.25
Outputs:
- grid: float32 [8, 128, 16, 512], P(('groups', 'tm'), 'chan'), parts along dimension 0
There are 2 independent parts, one for each index of `groups`. A program takes and returns all parts, laid end to end along the dimension named above; each array names one. Nothing has to cross between parts.
Inputs may be any that keep to these rules, and one draw needn't show every extreme that they name: `w_bin`: within the blocks of one device (aligned blocks of 32 along the channel-group and block dimensions taken together), no w-plane is named more than 16 times, a bound that some block reaches.
All inputs are finite; a program needn't handle non-finite values.
Results may differ from a plain program's by a relative error of at most 0.0041.
Values may be sent and summed in bfloat16 or wider, within the bound.
A program may use at most 128 MiB of HBM per device.

v0:
```python
import functools
import jax
import jax.numpy as jnp
from jax import lax
from jax.experimental import pallas as pl
from jax.experimental.pallas import tpu as pltpu
from jax.sharding import PartitionSpec as P

QW = 256
GC = 4096
MESH = pl.DeviceIdType.MESH
LIMIT = 63 * 1024 * 1024
TURNS = 16
PIECES = 4
LAG = 4


def pair_of(me):
    return me + 1 - 2 * (me % 2)


def write_table(table, bins, spots, cells, tiles):
    count = bins.shape[1]
    down = lax.broadcasted_iota(jnp.int32, (count, count), 0)
    along = lax.broadcasted_iota(jnp.int32, (count, count), 1)
    flat = jnp.broadcast_to(bins * tiles + spots, (count, count))
    tall = jnp.max(jnp.where(down == along, flat, 0), axis=1, keepdims=True)
    before = jnp.max(jnp.where((tall == flat) & (down < along), down + 1, 0), axis=0, keepdims=True)
    table[...] = jnp.zeros(table.shape, jnp.int32)
    table[0:1, 0:count] = before
    deep = lax.broadcasted_iota(jnp.int32, (count, 128), 0)
    wide = lax.broadcasted_iota(jnp.int32, (count, 128), 1)
    for r in range(-(-cells // 128)):
        named = tall == wide + r * 128
        table[1 + r:2 + r, :] = jnp.max(jnp.where(named, deep + 1, 0), axis=0, keepdims=True)


def exchange_kernel(
    planes, tiles, turns, bins, spots, vis, rows, cols, kern, out,
    bins_v, spots_v, tab_s, tab_v, vis_v, rows_v, cols_v, kern_v, runs, xout, xgot, zgot,
    lsem, ssend, srecv, xsend, xrecv, zsend, zrecv,
):
    me, mine = lax.axis_index("chan"), lax.axis_index("tm")
    core, row = me % 2, me // 2
    other = pair_of(me)
    count, fold, share = rows_v.shape[1], rows_v.shape[2], rows_v.shape[3]
    size = tiles // turns

    def x_peer(d):
        return {"chan": ((row + d) % fold) * 2 + core}

    def z_peer(d):
        return {"tm": (mine + d) % planes}

    local = [
        pltpu.make_async_copy(src, dst, lsem.at[i])
        for i, (src, dst) in enumerate((
            (bins, bins_v), (spots, spots_v), (vis, vis_v.at[0]), (rows.at[:, :, core], rows_v.at[0]),
            (cols, cols_v.at[0]), (kern, kern_v),
        ))
    ]
    for copy in local:
        copy.start()

    for copy in local[:2]:
        copy.wait()
    write_table(tab_v.at[0], bins_v[...], spots_v[...], planes * tiles, tiles)

    barrier = pltpu.get_barrier_semaphore()
    pl.semaphore_signal(barrier, inc=1, device_id={"chan": other}, device_id_type=MESH)
    for d in range(1, fold):
        pl.semaphore_signal(barrier, inc=1, device_id=x_peer(d), device_id_type=MESH)

    def hail(d, carry):
        pl.semaphore_signal(barrier, inc=1, device_id=z_peer(d), device_id_type=MESH)
        return carry
    lax.fori_loop(1, planes, hail, 0)
    pl.semaphore_wait(barrier, fold + planes - 1)

    piece = count // PIECES
    moves = [(vis, vis_v.at[1]), (tab_v.at[0], tab_v.at[1])]
    for p in range(PIECES):
        cut = pl.ds(p * piece, piece)
        moves += [(rows.at[cut, :, other % 2], rows_v.at[1, cut]), (cols.at[cut], cols_v.at[1, cut])]
    swaps = [
        pltpu.make_async_remote_copy(
            src_ref=src, dst_ref=dst, send_sem=ssend.at[i], recv_sem=srecv.at[i],
            device_id={"chan": other}, device_id_type=MESH,
        )
        for i, (src, dst) in enumerate(moves)
    ]
    for copy in swaps:
        copy.start()
    tables = [pltpu.make_async_copy(tab_v.at[i], tab_s.at[i], lsem.at[6 + i]) for i in range(2)]
    tables[0].start()

    for s in range(2):
        runs[s, 0] = jnp.zeros(runs.shape[2:], runs.dtype)

    def entry(s, i):
        return tab_s[s, i // 128, i % 128]

    batch = 4 if piece % 4 == 0 else 1

    def build(s, x, start, stop):
        def step(i, carry):
            found = []
            for u in range(batch):
                b = i * batch + u
                block = rows_v[s, b, x]
                weighted = jnp.concatenate(
                    [block * vis_v[s, b, 0:1, :], block * vis_v[s, b, 1:2, :]], axis=0
                )
                found.append(jnp.dot(weighted, cols_v[s, b], preferred_element_type=jnp.float32))
            for u in range(batch):
                b = i * batch + u
                last = entry(s, b)
                runs[s, b + 1, :, 0:QW] = found[u][:share] + runs[s, last, :, 0:QW]
                runs[s, b + 1, :, QW:2 * QW] = found[u][share:] + runs[s, last, :, QW:2 * QW]
            return carry
        lax.fori_loop(start // batch, stop // batch, step, 0)

    def cell(w, t):
        i = 128 + w * tiles + t
        return runs[0, entry(0, i)] + runs[1, entry(1, i)]

    def x_copy(j, d):
        cut = pl.ds(j * size, size)
        return pltpu.make_async_remote_copy(
            src_ref=xout.at[d - 1, :, cut], dst_ref=xgot.at[d - 1, :, cut],
            send_sem=xsend.at[j, d - 1], recv_sem=xrecv.at[j, d - 1],
            device_id=x_peer(d), device_id_type=MESH,
        )

    def z_copy(j, d):
        cut = pl.ds(j * size, size)
        return pltpu.make_async_remote_copy(
            src_ref=xgot.at[0, (mine + d) % planes, cut], dst_ref=zgot.at[d - 1, cut],
            send_sem=zsend.at[j, d - 1], recv_sem=zrecv.at[j, d - 1],
            device_id=z_peer(d), device_id_type=MESH,
        )

    for copy in local[2:5] + tables[:1]:
        copy.wait()
    for d in range(1, fold):
        half = (row + d) % fold
        build(0, half, 0, count)
        if d == 1:
            for copy in swaps[:2]:
                copy.wait_recv()
            tables[1].start()
            tables[1].wait()
        for p in range(PIECES):
            if d == 1:
                for copy in swaps[2 + 2 * p:4 + 2 * p]:
                    copy.wait_recv()
            build(1, half, p * piece, (p + 1) * piece)
        for j in range(turns):
            def fill(w, carry):
                for t in range(j * size, (j + 1) * size):
                    xout[d - 1, w, t] = cell(w, t).astype(xout.dtype)
                return carry
            lax.fori_loop(0, planes, fill, 0)
            x_copy(j, d).start()
    build(0, row, 0, count)
    build(1, row, 0, count)

    def over_x(w, t):
        total = cell(w, t)
        for d in range(1, fold):
            total = total + xgot[d - 1, w, t].astype(jnp.float32)
        return total

    def finish(j):
        def arrive(d, carry):
            z_copy(j, d).wait_recv()
            return carry
        lax.fori_loop(1, planes, arrive, 0)
        for t in range(j * size, (j + 1) * size):
            def add(d, total):
                return total + zgot[d - 1, t].astype(jnp.float32)
            total = lax.fori_loop(1, planes, add, over_x(mine, t), unroll=planes <= 4)
            out[:, t, :] = jnp.dot(total.astype(jnp.bfloat16), kern_v[...], preferred_element_type=jnp.float32)

    local[5].wait()
    for j in range(turns):
        for d in range(1, fold):
            x_copy(j, d).wait_recv()

        def forward(d, carry):
            w = (mine + d) % planes
            for t in range(j * size, (j + 1) * size):
                xgot[0, w, t] = over_x(w, t).astype(xgot.dtype)
            z_copy(j, d).start()
            return carry
        lax.fori_loop(1, planes, forward, 0)
        if j >= LAG:
            finish(j - LAG)

    for j in range(max(turns - LAG, 0), turns):
        finish(j)

    for copy in swaps:
        copy.wait_send()
    for j in range(turns):
        for d in range(1, fold):
            x_copy(j, d).wait_send()

        def leave(d, carry):
            z_copy(j, d).wait_send()
            return carry
        lax.fori_loop(1, planes, leave, 0)


def exchange(bins, spots, vis, rows, cols, kern, planes, tiles, turns):
    count, fold, _, share, width = rows.shape
    wide = 2 * cols.shape[2]
    any_spec = pl.BlockSpec(memory_space=pltpu.HBM)
    half = jnp.bfloat16
    dma = pltpu.SemaphoreType.DMA
    table = (-(-(1 + -(-planes * tiles // 128)) // 8) * 8, 128)
    grids = (2 * (fold - 1) * planes + planes - 1 + 2) * tiles * share * wide * 2
    held = 2 * (2 * cols.size + rows.size) + kern.size * 2 + 8 * (count + 1) * share * wide
    limit = min(LIMIT, grids + held + 6 * 1024 * 1024)
    return pl.pallas_call(
        functools.partial(exchange_kernel, planes, tiles, turns),
        out_shape=jax.ShapeDtypeStruct((share, tiles, wide), jnp.float32),
        in_specs=[any_spec] * 6,
        out_specs=pl.BlockSpec(memory_space=pltpu.VMEM),
        scratch_shapes=[
            pltpu.VMEM(bins.shape, jnp.int32),
            pltpu.VMEM(spots.shape, jnp.int32),
            pltpu.SMEM((2,) + table, jnp.int32),
            pltpu.VMEM((2,) + table, jnp.int32),
            pltpu.VMEM((2,) + vis.shape, vis.dtype),
            pltpu.VMEM((2, count, fold, share, width), rows.dtype),
            pltpu.VMEM((2,) + cols.shape, cols.dtype),
            pltpu.VMEM(kern.shape, kern.dtype),
            pltpu.VMEM((2, count + 1, share, wide), jnp.float32),
            pltpu.VMEM((fold - 1, planes, tiles, share, wide), half),
            pltpu.VMEM((fold - 1, planes, tiles, share, wide), half),
            pltpu.VMEM((planes - 1, tiles, share, wide), half),
            dma((8,)),
            dma((2 + 2 * PIECES,)),
            dma((2 + 2 * PIECES,)),
            dma((turns, fold - 1)),
            dma((turns, fold - 1)),
            dma((turns, planes - 1)),
            dma((turns, planes - 1)),
        ],
        compiler_params=pltpu.CompilerParams(
            collective_id=0, has_side_effects=True, vmem_limit_bytes=limit
        ),
        name="exchange",
    )(bins, spots, vis, rows, cols, kern)


def body(vis, row_weight, col_weight, w_bin, tile_col, w_kernel):
    planes = lax.axis_size("tm")
    chans = lax.axis_size("chan")
    count, rows_k, width_v = row_weight.shape[1:]
    tile_count = GC // QW
    fold = chans // 2
    bins = w_bin.reshape(1, count)
    rows = row_weight[0].reshape(count, fold, 2, rows_k // chans, width_v)
    result = exchange(bins, tile_col, vis[0], rows, col_weight[0], w_kernel[0], planes, tile_count, TURNS)
    return result[None]


def solution(mesh):
    in_specs = (
        P(("groups", "chan"), "tm", None, None),
        P(("groups", "chan"), "tm", None, None),
        P(("groups", "chan"), "tm", None, None),
        P(("groups", "chan"), "tm", None),
        P(("groups", "chan"), "tm"),
        P(("groups", "tm"), None, None),
    )
    out_specs = P(("groups", "tm"), "chan", None, None)
    return jax.shard_map(body, mesh=mesh, in_specs=in_specs, out_specs=out_specs, check_vma=False)
```

profile of v0, /device:TPU:0, one launch (start us, length us, event | category | flops | bytes accessed | tf_op | source)
XLA Modules:
  0.0 70.7 jit_solution(12393397321428015840)
XLA Ops:
  0.0 0.0 copy-start
  0.0 1.6 %copy-done = bf16[1,32,128,256]{3,2,1,0:T(8,128)(2,1)S(1)} copy-done((bf16[1,32,128,256]{3,2,1,0:T(8,128)(2,1)S(1)}, bf16[1,32,128,256]{3,2,1,0:T(8,128)(2,1)}, u32[]{:S(2)}) %copy-start) | copy-done | bytes 2097176
  1.6 0.0 copy-start.1
  1.6 1.2 %copy-done.1 = bf16[1,32,128,128]{3,2,1,0:T(8,128)(2,1)S(1)} copy-done((bf16[1,32,128,128]{3,2,1,0:T(8,128)(2,1)S(1)}, bf16[1,32,128,128]{3,2,1,0:T(8,128)(2,1)}, u32[]{:S(2)}) %copy-start.1) | copy-done | bytes 1048600
  2.8 0.0 copy-start.2
  2.8 1.0 %copy-done.2 = bf16[1,512,512]{2,1,0:T(8,128)(2,1)S(1)} copy-done((bf16[1,512,512]{2,1,0:T(8,128)(2,1)S(1)}, bf16[1,512,512]{2,1,0:T(8,128)(2,1)}, u32[]{:S(2)}) %copy-start.2) | copy-done | bytes 524312
  3.9 0.0 copy-start.3
  3.9 0.7 %copy-done.3 = bf16[1,32,2,128]{3,2,1,0:T(2,128)(2,1)S(1)} copy-done((bf16[1,32,2,128]{3,2,1,0:T(2,128)(2,1)S(1)}, bf16[1,32,2,128]{3,2,1,0:T(2,128)(2,1)}, u32[]{:S(2)}) %copy-start.3) | copy-done | bytes 16408
  4.6 0.0 copy-start.4
  4.6 0.7 copy-done.4
  5.2 0.0 copy-start.5
  5.2 0.7 copy-done.5
  5.9 63.8 %exchange.1 = f32[32,16,512]{2,1,0:T(8,128)S(1)} custom-call(s32[1,32]{1,0:T(1,128)S(1)} %bitcast.11, s32[1,32]{1,0:T(1,128)S(1)} %copy-done.5, bf16[32,2,128]{2,1,0:T(2,128)(2,1)S(1)} %bitcast.10, bf16[32,2,2,32,128]{4,3,2,1,0:T(8,128)(2,1)S(1)} %bitcast.8, bf16[32,128,256]{2,1,0:T(8,128)(2,1)S(1)} %bitcast.7, bf16[512,512]{1,0:T(8,128)(2,1)S(1)} %bitcast.9), custom_call_target="tpu_custom_call" | custom-call | tf_op jit(solution)/shard_map/exchange/pallas_call | solution.py:225
  69.7 1.0 %copy.8 = f32[1,32,16,512]{3,2,1,0:T(8,128)} copy(f32[1,32,16,512]{3,2,1,0:T(8,128)S(1)} %bitcast.6) | data formatting | bytes 2097152
Async XLA Ops:
  0.0 1.6 %copy-start = (bf16[1,32,128,256]{3,2,1,0:T(8,128)(2,1)S(1)}, bf16[1,32,128,256]{3,2,1,0:T(8,128)(2,1)}, u32[]{:S(2)}) copy-start(bf16[1,32,128,256]{3,2,1,0:T(8,128)(2,1)} %param.8) | copy-start | bytes 6291460
  1.6 1.2 %copy-start.1 = (bf16[1,32,128,128]{3,2,1,0:T(8,128)(2,1)S(1)}, bf16[1,32,128,128]{3,2,1,0:T(8,128)(2,1)}, u32[]{:S(2)}) copy-start(bf16[1,32,128,128]{3,2,1,0:T(8,128)(2,1)} %param.7) | copy-start | bytes 3145732
  2.8 1.0 %copy-start.2 = (bf16[1,512,512]{2,1,0:T(8,128)(2,1)S(1)}, bf16[1,512,512]{2,1,0:T(8,128)(2,1)}, u32[]{:S(2)}) copy-start(bf16[1,512,512]{2,1,0:T(8,128)(2,1)} %param.11) | copy-start | bytes 1572868
  3.9 0.7 %copy-start.3 = (bf16[1,32,2,128]{3,2,1,0:T(2,128)(2,1)S(1)}, bf16[1,32,2,128]{3,2,1,0:T(2,128)(2,1)}, u32[]{:S(2)}) copy-start(bf16[1,32,2,128]{3,2,1,0:T(2,128)(2,1)} %param.6) | copy-start | bytes 49156
  4.6 0.7 copy-start.4
  5.2 0.7 copy-start.5
where the time goes:
time: 71 us; the launch traced here: 70.7 us
  Pallas kernels  63.8 us (90%)
  local copies, waits for them, and re-layouts  6.85 us (10%)
    pallas_call x1, Pallas kernels, exchange(): pl.pallas_call(functools.partial(exchange_kernel, planes, tiles, turns),...  63.8 us
    unnamed x13, local copies, waits for them, and re-layouts  6.85 us

commit v1 on v0

v1 whole, which is shorter than its diff:
```python
import functools
import jax
import jax.numpy as jnp
from jax import lax
from jax.experimental import pallas as pl
from jax.experimental.pallas import tpu as pltpu
from jax.sharding import PartitionSpec as P

QW = 256
GC = 4096
MESH = pl.DeviceIdType.MESH
LIMIT = 63 * 1024 * 1024
GROUPS = 8
PIECES = 4
NEAR = 0
HOP = 0


def flip(z, k, planes):
    total, bit = 0, 1
    while bit < planes:
        total = total + ((z // bit + k // bit) % 2) * bit
        bit = 2 * bit
    return total


def write_table(table, bins, spots, cells, tiles):
    count = bins.shape[1]
    down = lax.broadcasted_iota(jnp.int32, (count, count), 0)
    along = lax.broadcasted_iota(jnp.int32, (count, count), 1)
    flat = jnp.broadcast_to(bins * tiles + spots, (count, count))
    tall = jnp.max(jnp.where(down == along, flat, 0), axis=1, keepdims=True)
    before = jnp.max(jnp.where((tall == flat) & (down < along), down + 1, 0), axis=0, keepdims=True)
    table[...] = jnp.zeros(table.shape, jnp.int32)
    table[0:1, 0:count] = before
    deep = lax.broadcasted_iota(jnp.int32, (count, 128), 0)
    wide = lax.broadcasted_iota(jnp.int32, (count, 128), 1)
    for r in range(-(-cells // 128)):
        named = tall == wide + r * 128
        table[1 + r:2 + r, :] = jnp.max(jnp.where(named, deep + 1, 0), axis=0, keepdims=True)


def loop(start, stop, step):
    def body(i, carry):
        step(i)
        return carry
    lax.fori_loop(start, stop, body, 0)


def over_planes(start, stop, step):
    if stop - start <= 4:
        for k in range(stop - 1, start - 1, -1):
            step(k)
    else:
        loop(0, stop - start, lambda i: step(stop - 1 - i))


def exchange_kernel(
    planes, tiles, groups, near, hop, bins, spots, vis, rows, cols, kern, out,
    bins_v, spots_v, tab_s, tab_v, vis_v, rows_v, cols_v, kern_v, runs, dout, dgot, xout, xgot, zgot, ngot, hgot,
    lsem, psem, ssend, srecv, dsend, drecv, xsend, xrecv, zsend, zrecv, nsend, nrecv, hsend, hrecv,
):
    me, mine = lax.axis_index("chan"), lax.axis_index("tm")
    core, row = me % 2, me // 2
    pair = {"chan": row * 2 + 1 - core}
    across = {"chan": (1 - row) * 2 + core}
    count, share = rows_v.shape[0], rows_v.shape[3]
    size = tiles // groups
    piece = count // PIECES
    half = xout.dtype

    def plane(k):
        return flip(mine, k, planes)

    small = [
        pltpu.make_async_copy(src, dst, lsem.at[i])
        for i, (src, dst) in enumerate(((bins, bins_v), (spots, spots_v), (vis, vis_v), (kern, kern_v)))
    ]
    parts = []
    for p in range(PIECES):
        cut = pl.ds(p * piece, piece)
        parts.append([
            pltpu.make_async_copy(rows.at[cut], rows_v.at[cut], psem.at[0, p]),
            pltpu.make_async_copy(cols.at[cut], cols_v.at[cut], psem.at[1, p]),
        ])
    for copy in small[:3] + sum(parts, []) + small[3:]:
        copy.start()

    barrier = pltpu.get_barrier_semaphore()
    pl.semaphore_signal(barrier, inc=1, device_id=pair, device_id_type=MESH)
    pl.semaphore_signal(barrier, inc=1, device_id=across, device_id_type=MESH)
    loop(1, planes, lambda k: pl.semaphore_signal(barrier, inc=1, device_id={"tm": plane(k)}, device_id_type=MESH))

    for copy in small[:2]:
        copy.wait()
    write_table(tab_v.at[0], bins_v[...], spots_v[...], planes * tiles, tiles)
    tables = [pltpu.make_async_copy(tab_v.at[i], tab_s.at[i], lsem.at[4 + i]) for i in range(2)]
    tables[0].start()
    swap = pltpu.make_async_remote_copy(
        src_ref=tab_v.at[0], dst_ref=tab_v.at[1], send_sem=ssend, recv_sem=srecv, device_id=pair, device_id_type=MESH,
    )
    for s in range(2):
        runs[s, 0] = jnp.zeros(runs.shape[2:], runs.dtype)

    def entry(s, i):
        return tab_s[s, i // 128, i % 128]

    def d_copy(s, p):
        cut = pl.ds(p * piece, piece)
        return pltpu.make_async_remote_copy(
            src_ref=dout.at[s, cut], dst_ref=dgot.at[s, cut], send_sem=dsend.at[s, p], recv_sem=drecv.at[s, p],
            device_id=pair, device_id_type=MESH,
        )

    def chain(s, b, found):
        last = entry(s, b)
        runs[s, b + 1, :, 0:QW] = found[:share] + runs[s, last, :, 0:QW]
        runs[s, b + 1, :, QW:2 * QW] = found[share:] + runs[s, last, :, QW:2 * QW]

    batch = 2 if piece % 2 == 0 else 1

    def build(s, x, p):
        def step(i):
            found = []
            for u in range(batch):
                b = p * piece + i * batch + u
                own, other = rows_v[b, x, core], rows_v[b, x, 1 - core]
                real, imag = vis_v[b, 0:1, :], vis_v[b, 1:2, :]
                weighted = jnp.concatenate([own * real, own * imag, other * real, other * imag], axis=0)
                found.append(jnp.dot(weighted, cols_v[b], preferred_element_type=jnp.float32))
            for u in range(batch):
                b = p * piece + i * batch + u
                dout[s, b] = found[u][2 * share:].astype(half)
                chain(0, b, found[u][:2 * share])
        loop(0, piece // batch, step)

    def join(s, p):
        def step(i):
            for u in range(batch):
                b = p * piece + i * batch + u
                chain(1, b, dgot[s, b].astype(jnp.float32))
        loop(0, piece // batch, step)

    def cell(w, t):
        i = 128 + w * tiles + t
        return runs[0, entry(0, i)] + runs[1, entry(1, i)]

    def cut_of(g):
        return pl.ds(g * size, size)

    def x_copy(k, g):
        w = plane(k)
        return pltpu.make_async_remote_copy(
            src_ref=xout.at[w, cut_of(g)], dst_ref=xgot.at[w, cut_of(g)],
            send_sem=xsend.at[k, g], recv_sem=xrecv.at[k, g], device_id=across, device_id_type=MESH,
        )

    def z_copy(k, g):
        w = plane(k)
        return pltpu.make_async_remote_copy(
            src_ref=xgot.at[w, cut_of(g)], dst_ref=zgot.at[k - 1, cut_of(g)],
            send_sem=zsend.at[k - 1, g], recv_sem=zrecv.at[k - 1, g], device_id={"tm": w}, device_id_type=MESH,
        )

    small[2].wait()
    tables[0].wait()
    for p in range(PIECES):
        for copy in parts[p]:
            copy.wait()
        build(0, 1 - row, p)
        if p == 0:
            pl.semaphore_wait(barrier, planes + 1)
            swap.start()
        d_copy(0, p).start()
    swap.wait_recv()
    tables[1].start()
    tables[1].wait()
    for p in range(PIECES):
        d_copy(0, p).wait_recv()
        join(0, p)

    def fill(k, g):
        w = plane(k)
        for u in range(size):
            t = g * size + u
            xout[w, t] = cell(w, t).astype(half)

    def send(k, g):
        fill(k, g)
        x_copy(k, g).start()

    over_planes(1, planes, lambda k: loop(0, groups, lambda g: send(k, g)))
    loop(0, groups, lambda g: send(0, g))

    for p in range(PIECES):
        build(1, row, p)
        d_copy(1, p).start()
    for p in range(PIECES):
        d_copy(1, p).wait_recv()
        join(1, p)

    def forward(k, g):
        w = plane(k)
        x_copy(k, g).wait_recv()
        for u in range(size):
            t = g * size + u
            xgot[w, t] = (cell(w, t) + xgot[w, t].astype(jnp.float32)).astype(half)
        z_copy(k, g).start()

    over_planes(1, planes, lambda k: loop(0, groups, lambda g: forward(k, g)))
    small[3].wait()

    def finish(g):
        x_copy(0, g).wait_recv()
        loop(1, planes, lambda k: z_copy(k, g).wait_recv())
        found = []
        for u in range(size):
            t = g * size + u
            total = cell(mine, t) + xgot[mine, t].astype(jnp.float32)

            def add(k, total):
                return total + zgot[k - 1, t].astype(jnp.float32)
            found.append(lax.fori_loop(1, planes, add, total, unroll=planes <= 4).astype(jnp.bfloat16))
        done = jnp.dot(jnp.concatenate(found, axis=0), kern_v[...], preferred_element_type=jnp.float32)
        for u in range(size):
            out[:, g * size + u, :] = done[u * share:(u + 1) * share]

    for g in range(groups):
        finish(g)

    swap.wait_send()
    for s in range(2):
        for p in range(PIECES):
            d_copy(s, p).wait_send()

    def leave(g):
        loop(0, planes, lambda k: x_copy(k, g).wait_send())
        loop(1, planes, lambda k: z_copy(k, g).wait_send())
    loop(0, groups, leave)


def exchange(bins, spots, vis, rows, cols, kern, planes, tiles):
    count, fold, _, share, width = rows.shape
    wide = 2 * cols.shape[2]
    groups = GROUPS
    near, hop = (NEAR, HOP) if planes == 4 else (0, 0)
    size = tiles // groups
    any_spec = pl.BlockSpec(memory_space=pltpu.HBM)
    half = jnp.bfloat16
    dma = pltpu.SemaphoreType.DMA
    table = (-(-(1 + -(-planes * tiles // 128)) // 8) * 8, 128)
    return pl.pallas_call(
        functools.partial(exchange_kernel, planes, tiles, groups, near, hop),
        out_shape=jax.ShapeDtypeStruct((share, tiles, wide), jnp.float32),
        in_specs=[any_spec] * 6,
        out_specs=pl.BlockSpec(memory_space=pltpu.VMEM),
        scratch_shapes=[
            pltpu.VMEM(bins.shape, jnp.int32),
            pltpu.VMEM(spots.shape, jnp.int32),
            pltpu.SMEM((2,) + table, jnp.int32),
            pltpu.VMEM((2,) + table, jnp.int32),
            pltpu.VMEM(vis.shape, vis.dtype),
            pltpu.VMEM(rows.shape, rows.dtype),
            pltpu.VMEM(cols.shape, cols.dtype),
            pltpu.VMEM(kern.shape, kern.dtype),
            pltpu.VMEM((2, count + 1, share, wide), jnp.float32),
            pltpu.VMEM((2, count, 2 * share, wide // 2), half),
            pltpu.VMEM((2, count, 2 * share, wide // 2), half),
            pltpu.VMEM((planes, tiles, share, wide), half),
            pltpu.VMEM((planes, tiles, share, wide), half),
            pltpu.VMEM((planes - 1, tiles, share, wide), half),
            pltpu.VMEM((max(near, 1) * size, share, wide), half),
            pltpu.VMEM((max(hop, 1) * size, share, wide), half),
            dma((6,)),
            dma((2, PIECES)),
            dma,
            dma,
            dma((2, PIECES)),
            dma((2, PIECES)),
            dma((planes, groups)),
            dma((planes, groups)),
            dma((planes - 1, groups)),
            dma((planes - 1, groups)),
            dma((max(near, 1),)),
            dma((max(near, 1),)),
            dma((max(hop, 1),)),
            dma((max(hop, 1),)),
        ],
        compiler_params=pltpu.CompilerParams(
            collective_id=0, has_side_effects=True, vmem_limit_bytes=LIMIT
        ),
        name="exchange",
    )(bins, spots, vis, rows, cols, kern)


def body(vis, row_weight, col_weight, w_bin, tile_col, w_kernel):
    planes = lax.axis_size("tm")
    chans = lax.axis_size("chan")
    count, rows_k, width_v = row_weight.shape[1:]
    tile_count = GC // QW
    fold = chans // 2
    bins = w_bin.reshape(1, count)
    rows = row_weight[0].reshape(count, fold, 2, rows_k // chans, width_v)
    result = exchange(bins, tile_col, vis[0], rows, col_weight[0], w_kernel[0], planes, tile_count)
    return result[None]


def solution(mesh):
    in_specs = (
        P(("groups", "chan"), "tm", None, None),
        P(("groups", "chan"), "tm", None, None),
        P(("groups", "chan"), "tm", None, None),
        P(("groups", "chan"), "tm", None),
        P(("groups", "chan"), "tm"),
        P(("groups", "tm"), None, None),
    )
    out_specs = P(("groups", "tm"), "chan", None, None)
    return jax.shard_map(body, mesh=mesh, in_specs=in_specs, out_specs=out_specs, check_vma=False)
```

time: 71 us -> 67 us (0.944)
  local copies, waits for them, and re-layouts: 6.85 us -> 2.31 us
  Pallas kernels: 63.8 us -> 64.6 us
    unnamed x13 -> x1, local copies, waits for them, and re-layouts: 6.85 us -> 2.31 us
    pallas_call x1, Pallas kernels: 63.8 us -> 64.6 us  [exchange(): pl.pallas_call(functools.partial(exchange_kernel, planes, tiles, groups,...]
where the time goes in v1:
time: 67 us; the launch traced here: 66.9 us
  Pallas kernels  64.6 us (96%)
  local copies, waits for them, and re-layouts  2.31 us (3%)
    pallas_call x1, Pallas kernels, exchange(): pl.pallas_call(functools.partial(exchange_kernel, planes, tiles, groups,...  64.6 us
    unnamed x1, local copies, waits for them, and re-layouts  2.31 us

profile of v1, /device:TPU:0, one launch (start us, length us, event | category | flops | bytes accessed | tf_op | source)
XLA Modules:
  0.0 66.9 jit_solution(1664958677115203407)
XLA Ops:
  0.0 64.6 %exchange.1 = f32[32,16,512]{2,1,0:T(8,128)} custom-call(s32[1,32]{1,0:T(1,128)} %bitcast.11, s32[1,32]{1,0:T(1,128)} %spots.1, bf16[32,2,128]{2,1,0:T(2,128)(2,1)} %bitcast.10, bf16[32,2,2,32,128]{4,3,2,1,0:T(8,128)(2,1)} %bitcast.8, bf16[32,128,256]{2,1,0:T(8,128)(2,1)} %bitcast.7, bf16[512,512]{1,0:T(8,128)(2,1)} %bitcast.9), custom_call_target="tpu_custom_call" | custom-call | tf_op jit(solution)/shard_map/exchange/pallas_call | solution.py:252
  64.6 2.3 %copy.8 = f32[1,32,16,512]{3,2,1,0:T(8,128)} copy(f32[1,32,16,512]{3,2,1,0:T(8,128)} %bitcast.6) | data formatting | bytes 2097152

commit v2 on v1

--- a/solution.py
+++ b/solution.py
@@ -12,8 +12,8 @@
 LIMIT = 63 * 1024 * 1024
 GROUPS = 8
 PIECES = 4
-NEAR = 0
-HOP = 0
+NEAR = 4
+HOP = 4
 
 
 def flip(z, k, planes):
@@ -68,6 +68,7 @@
     size = tiles // groups
     piece = count // PIECES
     half = xout.dtype
+    edge = mine % (planes - 1) == 0
 
     def plane(k):
         return flip(mine, k, planes)
@@ -91,16 +92,17 @@
     pl.semaphore_signal(barrier, inc=1, device_id=across, device_id_type=MESH)
     loop(1, planes, lambda k: pl.semaphore_signal(barrier, inc=1, device_id={"tm": plane(k)}, device_id_type=MESH))
 
-    for copy in small[:2]:
-        copy.wait()
-    write_table(tab_v.at[0], bins_v[...], spots_v[...], planes * tiles, tiles)
     tables = [pltpu.make_async_copy(tab_v.at[i], tab_s.at[i], lsem.at[4 + i]) for i in range(2)]
-    tables[0].start()
     swap = pltpu.make_async_remote_copy(
         src_ref=tab_v.at[0], dst_ref=tab_v.at[1], send_sem=ssend, recv_sem=srecv, device_id=pair, device_id_type=MESH,
     )
     for s in range(2):
         runs[s, 0] = jnp.zeros(runs.shape[2:], runs.dtype)
+    if hop:
+        @pl.when(edge)
+        def _():
+            zgot[planes - 2, pl.ds((groups - hop) * size, hop * size)] = jnp.zeros(hgot.shape, half)
+            hgot[...] = jnp.zeros(hgot.shape, half)
 
     def entry(s, i):
         return tab_s[s, i // 128, i % 128]
@@ -112,33 +114,33 @@
             device_id=pair, device_id_type=MESH,
         )
 
-    def chain(s, b, found):
-        last = entry(s, b)
-        runs[s, b + 1, :, 0:QW] = found[:share] + runs[s, last, :, 0:QW]
-        runs[s, b + 1, :, QW:2 * QW] = found[share:] + runs[s, last, :, QW:2 * QW]
-
-    batch = 2 if piece % 2 == 0 else 1
-
     def build(s, x, p):
+        found = []
+        for b in range(p * piece, (p + 1) * piece):
+            own, other = rows_v[b, x, core], rows_v[b, x, 1 - core]
+            real, imag = vis_v[b, 0:1, :], vis_v[b, 1:2, :]
+            weighted = jnp.concatenate([own * real, own * imag, other * real, other * imag], axis=0)
+            found = jnp.dot(weighted, cols_v[b], preferred_element_type=jnp.float32)
+            dout[s, b] = found[2 * share:].astype(half)
+            runs[0, b + 1, :, 0:QW] = found[:share]
+            runs[0, b + 1, :, QW:2 * QW] = found[share:2 * share]
+
+    batch = 4 if piece % 4 == 0 else 1
+
+    def chain(start, stop):
         def step(i):
-            found = []
             for u in range(batch):
-                b = p * piece + i * batch + u
-                own, other = rows_v[b, x, core], rows_v[b, x, 1 - core]
-                real, imag = vis_v[b, 0:1, :], vis_v[b, 1:2, :]
-                weighted = jnp.concatenate([own * real, own * imag, other * real, other * imag], axis=0)
-                found.append(jnp.dot(weighted, cols_v[b], preferred_element_type=jnp.float32))
-            for u in range(batch):
-                b = p * piece + i * batch + u
-                dout[s, b] = found[u][2 * share:].astype(half)
-                chain(0, b, found[u][:2 * share])
-        loop(0, piece // batch, step)
+                b = start + i * batch + u
+                runs[0, b + 1] = runs[0, b + 1] + runs[0, entry(0, b)]
+        loop(0, (stop - start) // batch, step)
 
     def join(s, p):
         def step(i):
             for u in range(batch):
                 b = p * piece + i * batch + u
-                chain(1, b, dgot[s, b].astype(jnp.float32))
+                found, last = dgot[s, b].astype(jnp.float32), entry(1, b)
+                runs[1, b + 1, :, 0:QW] = found[:share] + runs[1, last, :, 0:QW]
+                runs[1, b + 1, :, QW:2 * QW] = found[share:] + runs[1, last, :, QW:2 * QW]
         loop(0, piece // batch, step)
 
     def cell(w, t):
@@ -162,22 +164,51 @@
             send_sem=zsend.at[k - 1, g], recv_sem=zrecv.at[k - 1, g], device_id={"tm": w}, device_id_type=MESH,
         )
 
+    def near_copy(g):
+        cut = pl.ds((g - (groups - near)) * size, size)
+        return pltpu.make_async_remote_copy(
+            src_ref=xout.at[plane(1), cut_of(g)], dst_ref=ngot.at[cut],
+            send_sem=nsend.at[g - (groups - near)], recv_sem=nrecv.at[g - (groups - near)],
+            device_id={"tm": plane(1)}, device_id_type=MESH,
+        )
+
+    def hop_copy(g):
+        cut = pl.ds((g - (groups - hop)) * size, size)
+        return pltpu.make_async_remote_copy(
+            src_ref=xgot.at[plane(planes - 1), cut_of(g)], dst_ref=hgot.at[cut],
+            send_sem=hsend.at[g - (groups - hop)], recv_sem=hrecv.at[g - (groups - hop)],
+            device_id={"tm": plane(1)}, device_id_type=MESH,
+        )
+
     small[2].wait()
-    tables[0].wait()
     for p in range(PIECES):
-        for copy in parts[p]:
-            copy.wait()
-        build(0, 1 - row, p)
+        with jax.named_scope("load_wait"):
+            for copy in parts[p]:
+                copy.wait()
+        with jax.named_scope("build_far"):
+            build(0, 1 - row, p)
         if p == 0:
-            pl.semaphore_wait(barrier, planes + 1)
+            with jax.named_scope("write_table"):
+                for copy in small[:2]:
+                    copy.wait()
+                write_table(tab_v.at[0], bins_v[...], spots_v[...], planes * tiles, tiles)
+                tables[0].start()
+            with jax.named_scope("barrier"):
+                pl.semaphore_wait(barrier, planes + 1)
             swap.start()
         d_copy(0, p).start()
-    swap.wait_recv()
-    tables[1].start()
+    with jax.named_scope("table"):
+        swap.wait_recv()
+        tables[1].start()
+        tables[0].wait()
+    with jax.named_scope("chain_far"):
+        chain(0, count)
     tables[1].wait()
     for p in range(PIECES):
-        d_copy(0, p).wait_recv()
-        join(0, p)
+        with jax.named_scope("pair_wait"):
+            d_copy(0, p).wait_recv()
+        with jax.named_scope("join_far"):
+            join(0, p)
 
     def fill(k, g):
         w = plane(k)
@@ -189,30 +220,91 @@
         fill(k, g)
         x_copy(k, g).start()
 
-    over_planes(1, planes, lambda k: loop(0, groups, lambda g: send(k, g)))
-    loop(0, groups, lambda g: send(0, g))
+    with jax.named_scope("fill"):
+        def send_all(k):
+            shift = groups - hop if planes <= 4 and k == planes - 1 else 0
+            loop(0, groups, lambda i: send(k, (i + shift) % groups))
+            if near and k == planes - 1:
+                def approach(g):
+                    fill(1, g)
+                    near_copy(g).start()
+                loop(groups - near, groups, approach)
+        over_planes(2, planes, send_all)
+        for k in (1, 0):
+            loop(0, groups - near, lambda g: send(k, g))
+        loop(groups - near, groups, lambda g: fill(0, g))
 
     for p in range(PIECES):
-        build(1, row, p)
+        with jax.named_scope("build_near"):
+            build(1, row, p)
         d_copy(1, p).start()
+    with jax.named_scope("chain_near"):
+        chain(0, count)
     for p in range(PIECES):
-        d_copy(1, p).wait_recv()
-        join(1, p)
-
-    def forward(k, g):
+        with jax.named_scope("join_near"):
+            d_copy(1, p).wait_recv()
+            join(1, p)
+
+    def gather(k, g, crossed=True, hopped=False):
         w = plane(k)
-        x_copy(k, g).wait_recv()
+        if crossed:
+            x_copy(k, g).wait_recv()
+        if hopped:
+            pl.when(jnp.logical_not(edge))(lambda: hop_copy(g).wait_recv())
         for u in range(size):
             t = g * size + u
-            xgot[w, t] = (cell(w, t) + xgot[w, t].astype(jnp.float32)).astype(half)
+            total = cell(w, t)
+            if crossed:
+                total = total + xgot[w, t].astype(jnp.float32)
+            if hopped:
+                total = total + hgot[t - (groups - hop) * size].astype(jnp.float32)
+            xgot[w, t] = total.astype(half)
+
+    def forward(k, g, crossed=True, hopped=False):
+        gather(k, g, crossed, hopped)
         z_copy(k, g).start()
 
-    over_planes(1, planes, lambda k: loop(0, groups, lambda g: forward(k, g)))
+    def detour(g):
+        gather(planes - 1, g)
+        pl.when(edge)(lambda: hop_copy(g).start())
+        pl.when(jnp.logical_not(edge))(lambda: z_copy(planes - 1, g).start())
+
+    def merge(g):
+        near_copy(g).wait_recv()
+        for u in range(size):
+            t = g * size + u
+            arrived = ngot[t - (groups - near) * size].astype(jnp.float32)
+            xout[mine, t] = (xout[mine, t].astype(jnp.float32) + arrived).astype(half)
+        x_copy(0, g).start()
+
+    def forward_all(k):
+        with jax.named_scope("forward"):
+            if hop and k == planes - 1:
+                loop(groups - hop, groups, detour)
+                loop(0, groups - hop, lambda g: forward(k, g))
+            elif hop and k == planes - 2:
+                loop(0, groups - hop, lambda g: forward(k, g))
+                loop(groups - hop, groups, lambda g: forward(k, g, hopped=True))
+            else:
+                loop(0, groups, lambda g: forward(k, g))
+        if near and k == planes - 1:
+            with jax.named_scope("merge"):
+                loop(groups - near, groups, merge)
+    over_planes(2, planes, forward_all)
+    with jax.named_scope("forward"):
+        loop(0, groups - near, lambda g: forward(1, g))
+        loop(groups - near, groups, lambda g: forward(1, g, crossed=False))
     small[3].wait()
 
     def finish(g):
-        x_copy(0, g).wait_recv()
-        loop(1, planes, lambda k: z_copy(k, g).wait_recv())
+        with jax.named_scope("finish_x"):
+            x_copy(0, g).wait_recv()
+        with jax.named_scope("finish_z"):
+            loop(1, planes - 1, lambda k: z_copy(k, g).wait_recv())
+            if g < groups - hop:
+                z_copy(planes - 1, g).wait_recv()
+            else:
+                pl.when(jnp.logical_not(edge))(lambda: z_copy(planes - 1, g).wait_recv())
         found = []
         for u in range(size):
             t = g * size + u
@@ -226,7 +318,8 @@
             out[:, g * size + u, :] = done[u * share:(u + 1) * share]
 
     for g in range(groups):
-        finish(g)
+        with jax.named_scope("finish"):
+            finish(g)
 
     swap.wait_send()
     for s in range(2):
@@ -234,9 +327,18 @@
             d_copy(s, p).wait_send()
 
     def leave(g):
-        loop(0, planes, lambda k: x_copy(k, g).wait_send())
-        loop(1, planes, lambda k: z_copy(k, g).wait_send())
+        x_copy(0, g).wait_send()
+        loop(2, planes, lambda k: x_copy(k, g).wait_send())
+        loop(1, planes - 1, lambda k: z_copy(k, g).wait_send())
     loop(0, groups, leave)
+    loop(0, groups - near, lambda g: x_copy(1, g).wait_send())
+    loop(groups - near, groups, lambda g: near_copy(g).wait_send())
+    loop(0, groups - hop, lambda g: z_copy(planes - 1, g).wait_send())
+
+    def depart(g):
+        pl.when(edge)(lambda: hop_copy(g).wait_send())
+        pl.when(jnp.logical_not(edge))(lambda: z_copy(planes - 1, g).wait_send())
+    loop(groups - hop, groups, depart)
 
 
 def exchange(bins, spots, vis, rows, cols, kern, planes, tiles):
@@ -249,6 +351,10 @@
     half = jnp.bfloat16
     dma = pltpu.SemaphoreType.DMA
     table = (-(-(1 + -(-planes * tiles // 128)) // 8) * 8, 128)
+    grids = (2 * planes + planes - 1 + 2) * tiles * share * wide * 2
+    held = 2 * (rows.size + cols.size + kern.size) + 8 * (count + 1) * share * wide + 8 * count * share * wide
+    limit = min(LIMIT, grids + held + 6 * 1024 * 1024)
+    operands = [pltpu.with_memory_space_constraint(a, pltpu.HBM) for a in (bins, spots, vis, rows, cols, kern)]
     return pl.pallas_call(
         functools.partial(exchange_kernel, planes, tiles, groups, near, hop),
         out_shape=jax.ShapeDtypeStruct((share, tiles, wide), jnp.float32),
@@ -287,10 +393,10 @@
             dma((max(hop, 1),)),
         ],
         compiler_params=pltpu.CompilerParams(
-            collective_id=0, has_side_effects=True, vmem_limit_bytes=LIMIT
+            collective_id=0, has_side_effects=True, vmem_limit_bytes=limit
         ),
         name="exchange",
-    )(bins, spots, vis, rows, cols, kern)
+    )(*operands)
 
 
 def body(vis, row_weight, col_weight, w_bin, tile_col, w_kernel):

time: 67 us -> 61.3 us (0.915)
  Pallas kernels: 64.6 us -> 60.2 us
  local copies, waits for them, and re-layouts: 2.31 us -> 0.97 us
    pallas_call x1, Pallas kernels: 64.6 us -> 60.2 us  [exchange(): pl.pallas_call(functools.partial(exchange_kernel, planes, tiles, groups,...]
    unnamed x1, local copies, waits for them, and re-layouts: 2.31 us -> 0.97 us
where the time goes in v2:
time: 61.3 us; the launch traced here: 61.2 us
  Pallas kernels  60.2 us (98%)
  local copies, waits for them, and re-layouts  0.97 us (2%)
    pallas_call x1, Pallas kernels, exchange(): pl.pallas_call(functools.partial(exchange_kernel, planes, tiles, groups,...  60.2 us

profile of v2, /device:TPU:0, one launch (start us, length us, event | category | flops | bytes accessed | tf_op | source)
XLA Modules:
  0.0 61.2 jit_solution(2211878636365563151)
XLA Ops:
  0.0 60.2 %exchange.1 = f32[32,16,512]{2,1,0:T(8,128)S(1)} custom-call(s32[1,32]{1,0:T(1,128)} %bitcast.11, s32[1,32]{1,0:T(1,128)} %spots.1, bf16[32,2,128]{2,1,0:T(2,128)(2,1)} %bitcast.10, bf16[32,2,2,32,128]{4,3,2,1,0:T(8,128)(2,1)} %bitcast.8, bf16[32,128,256]{2,1,0:T(8,128)(2,1)} %bitcast.7, bf16[512,512]{1,0:T(8,128)(2,1)} %bitcast.9), custom_call_target="tpu_custom_call" | custom-call | tf_op jit(solution)/shard_map/exchange/pallas_call | solution.py:358
  60.2 1.0 %copy.8 = f32[1,32,16,512]{3,2,1,0:T(8,128)} copy(f32[1,32,16,512]{3,2,1,0:T(8,128)S(1)} %bitcast.6) | data formatting | bytes 2097152

commit v3 on v2

v3 whole, which is shorter than its diff:
```python
import functools
import jax
import jax.numpy as jnp
from jax import lax
from jax.experimental import pallas as pl
from jax.experimental.pallas import tpu as pltpu
from jax.sharding import PartitionSpec as P

QW = 256
GC = 4096
MESH = pl.DeviceIdType.MESH
LIMIT = 63 * 1024 * 1024
PARTS = 4
TURNS = 8
PIECES = 4
NEAR = 2


def write_table(table, bins, spots, cells, tiles):
    count = bins.shape[1]
    down = lax.broadcasted_iota(jnp.int32, (count, count), 0)
    along = lax.broadcasted_iota(jnp.int32, (count, count), 1)
    flat = jnp.broadcast_to(bins * tiles + spots, (count, count))
    tall = jnp.max(jnp.where(down == along, flat, 0), axis=1, keepdims=True)
    before = jnp.max(jnp.where((tall == flat) & (down < along), down + 1, 0), axis=0, keepdims=True)
    table[...] = jnp.zeros(table.shape, jnp.int32)
    table[0:1, 0:count] = before
    deep = lax.broadcasted_iota(jnp.int32, (count, 128), 0)
    wide = lax.broadcasted_iota(jnp.int32, (count, 128), 1)
    for r in range(-(-cells // 128)):
        named = tall == wide + r * 128
        table[1 + r:2 + r, :] = jnp.max(jnp.where(named, deep + 1, 0), axis=0, keepdims=True)


def loop(start, stop, step):
    def body(i, carry):
        step(i)
        return carry
    lax.fori_loop(start, stop, body, 0)


def over_planes(start, stop, step):
    if stop - start <= 4:
        for k in range(start, stop):
            step(k)
    else:
        loop(start, stop, step)


def exchange_kernel(
    planes, tiles, groups, turns, near, bins, spots, vis, rows, cols, kern, out,
    bins_v, spots_v, tab_s, tab_v, vis_v, rows_v, cols_v, kern_v, runs, dout, dgot, xout, xgot, zgot, ngot,
    lsem, psem, ssend, srecv, dsend, drecv, xsend, xrecv, yrecv, zsend, zrecv, nrecv,
):
    me, mine = lax.axis_index("chan"), lax.axis_index("tm")
    core, row = me % 2, me // 2
    pair = {"chan": row * 2 + 1 - core}
    across = {"chan": (1 - row) * 2 + core}
    count, share = rows_v.shape[0], rows_v.shape[3]
    size, step = tiles // groups, tiles // turns
    piece = count // PIECES
    half = xout.dtype
    edge = mine % (planes - 1) == 0

    up = mine // (planes // 2)
    reach = up * mine + (1 - up) * (planes - 1 - mine)
    beside = {"tm": mine + 1 - 2 * (mine % 2)}

    def less(a, b):
        return (planes - 1 + b - a) // planes

    def plane(i):
        late = i // reach
        v = (1 - late) * i + late * (planes - 1 - (i - reach))
        return up * v + (1 - up) * (planes - 1 - v)

    def slot(w):
        return w + less(w, mine) * (1 - less(w, mine - 1)) * (planes - w)

    small = [
        pltpu.make_async_copy(src, dst, lsem.at[i])
        for i, (src, dst) in enumerate(((bins, bins_v), (spots, spots_v), (vis, vis_v), (kern, kern_v)))
    ]
    parts = []
    for p in range(PIECES):
        cut = pl.ds(p * piece, piece)
        parts.append([
            pltpu.make_async_copy(rows.at[cut], rows_v.at[cut], psem.at[0, p]),
            pltpu.make_async_copy(cols.at[cut], cols_v.at[cut], psem.at[1, p]),
        ])
    for copy in small[:3] + sum(parts, []) + small[3:]:
        copy.start()

    barrier = pltpu.get_barrier_semaphore()
    pl.semaphore_signal(barrier, inc=1, device_id=pair, device_id_type=MESH)
    pl.semaphore_signal(barrier, inc=1, device_id=across, device_id_type=MESH)

    def greet(step):
        pl.semaphore_signal(barrier, inc=1, device_id={"tm": mine + step}, device_id_type=MESH)
    pl.when(mine > 0)(lambda: greet(-1))
    pl.when(mine < planes - 1)(lambda: greet(1))

    tables = [pltpu.make_async_copy(tab_v.at[i], tab_s.at[i], lsem.at[4 + i]) for i in range(2)]
    swap = pltpu.make_async_remote_copy(
        src_ref=tab_v.at[0], dst_ref=tab_v.at[1], send_sem=ssend, recv_sem=srecv, device_id=pair, device_id_type=MESH,
    )
    for s in range(2):
        runs[s, 0] = jnp.zeros(runs.shape[2:], runs.dtype)

    @pl.when(edge)
    def _():
        zgot[(mine // (planes - 1)) * planes] = jnp.zeros(zgot.shape[1:], half)

    def entry(s, i):
        return tab_s[s, i // 128, i % 128]

    def d_copy(s, p):
        cut = pl.ds(p * piece, piece)
        return pltpu.make_async_remote_copy(
            src_ref=dout.at[s, cut], dst_ref=dgot.at[s, cut], send_sem=dsend, recv_sem=drecv.at[s, p],
            device_id=pair, device_id_type=MESH,
        )

    def build(s, x, p):
        found = []
        for b in range(p * piece, (p + 1) * piece):
            own, other = rows_v[b, x, core], rows_v[b, x, 1 - core]
            real, imag = vis_v[b, 0:1, :], vis_v[b, 1:2, :]
            weighted = jnp.concatenate([own * real, own * imag, other * real, other * imag], axis=0)
            found = jnp.dot(weighted, cols_v[b], preferred_element_type=jnp.float32)
            dout[s, b] = found[2 * share:].astype(half)
            runs[0, b + 1, :, 0:QW] = found[:share]
            runs[0, b + 1, :, QW:2 * QW] = found[share:2 * share]

    batch = 4 if piece % 4 == 0 else 1

    def chain(start, stop):
        def step(i):
            for u in range(batch):
                b = start + i * batch + u
                runs[0, b + 1] = runs[0, b + 1] + runs[0, entry(0, b)]
        loop(0, (stop - start) // batch, step)

    def join(s, p):
        def step(i):
            for u in range(batch):
                b = p * piece + i * batch + u
                found, last = dgot[s, b].astype(jnp.float32), entry(1, b)
                runs[1, b + 1, :, 0:QW] = found[:share] + runs[1, last, :, 0:QW]
                runs[1, b + 1, :, QW:2 * QW] = found[share:] + runs[1, last, :, QW:2 * QW]
        loop(0, piece // batch, step)

    def cell(w, t):
        i = 128 + w * tiles + t
        return runs[0, entry(0, i)] + runs[1, entry(1, i)]

    later = turns - near * turns // groups

    def cut_of(g):
        return pl.ds(g * size, size)

    def x_copy(i, g):
        w = plane(i)
        return pltpu.make_async_remote_copy(
            src_ref=xout.at[w, cut_of(g)], dst_ref=xgot.at[w, cut_of(g)],
            send_sem=xsend, recv_sem=xrecv.at[i, g], device_id=across, device_id_type=MESH,
        )

    def y_copy(j):
        cut = pl.ds(j * step, step)
        return pltpu.make_async_remote_copy(
            src_ref=xout.at[mine, cut], dst_ref=xgot.at[mine, cut],
            send_sem=xsend, recv_sem=yrecv.at[j], device_id=across, device_id_type=MESH,
        )

    def z_copy(w, g):
        return pltpu.make_async_remote_copy(
            src_ref=xgot.at[w, cut_of(g)], dst_ref=zgot.at[slot(w), cut_of(g)],
            send_sem=zsend, recv_sem=zrecv.at[slot(w), g],
            device_id={"tm": mine + 2 * less(mine, w) - 1}, device_id_type=MESH,
        )

    def z_wait(at, g):
        pltpu.make_async_remote_copy(
            src_ref=xgot.at[0, cut_of(g)], dst_ref=zgot.at[at, cut_of(g)],
            send_sem=zsend, recv_sem=zrecv.at[at, g], device_id=beside, device_id_type=MESH,
        ).wait_recv()

    def near_copy(g):
        at = g - (groups - near)
        return pltpu.make_async_remote_copy(
            src_ref=xout.at[plane(planes - 2), cut_of(g)], dst_ref=ngot.at[pl.ds(at * size, size)],
            send_sem=xsend, recv_sem=nrecv.at[at], device_id=beside, device_id_type=MESH,
        )

    small[2].wait()
    for p in range(PIECES):
        with jax.named_scope("load_wait"):
            for copy in parts[p]:
                copy.wait()
        with jax.named_scope("build_far"):
            build(0, 1 - row, p)
        if p == 0:
            with jax.named_scope("write_table"):
                for copy in small[:2]:
                    copy.wait()
                write_table(tab_v.at[0], bins_v[...], spots_v[...], planes * tiles, tiles)
                tables[0].start()
            with jax.named_scope("barrier"):
                pl.semaphore_wait(barrier, 3 + less(0, mine) * less(mine, planes - 1))
            swap.start()
        d_copy(0, p).start()
    with jax.named_scope("table"):
        swap.wait_recv()
        tables[1].start()
        tables[0].wait()
    with jax.named_scope("chain_far"):
        chain(0, count)
    tables[1].wait()
    for p in range(PIECES):
        with jax.named_scope("pair_wait"):
            d_copy(0, p).wait_recv()
        with jax.named_scope("join_far"):
            join(0, p)

    def fill(w, start, many):
        for u in range(many):
            xout[w, start + u] = cell(w, start + u).astype(half)

    def send(i, g):
        fill(plane(i), g * size, size)
        x_copy(i, g).start()

    def send_own(j):
        fill(mine, j * step, step)
        y_copy(j).start()

    def approach(g):
        fill(plane(planes - 2), g * size, size)
        near_copy(g).start()

    with jax.named_scope("fill"):
        loop(0, groups, lambda g: send(0, g))
        loop(groups - near, groups, approach)
        over_planes(1, planes - 2, lambda i: loop(0, groups, lambda g: send(i, g)))
        loop(0, groups - near, lambda g: send(planes - 2, g))
        loop(0, later, send_own)
        loop(later, turns, lambda j: fill(mine, j * step, step))

    for p in range(PIECES):
        with jax.named_scope("build_near"):
            build(1, row, p)
        d_copy(1, p).start()
    with jax.named_scope("chain_near"):
        chain(0, count)
    for p in range(PIECES):
        with jax.named_scope("join_near"):
            d_copy(1, p).wait_recv()
            join(1, p)

    def gather(w, g, crossed, joined):
        for u in range(size):
            t = g * size + u
            total = cell(w, t)
            if crossed:
                total = total + xgot[w, t].astype(jnp.float32)
            if joined:
                total = total + zgot[w, t].astype(jnp.float32)
            xgot[w, t] = total.astype(half)

    def forward(i, g, joined, crossed=True):
        w = plane(i)
        if crossed:
            x_copy(i, g).wait_recv()
        if joined:
            z_wait(w, g)
        gather(w, g, crossed, joined)
        z_copy(w, g).start()

    def merge(g):
        near_copy(g).wait_recv()
        for u in range(size):
            t = g * size + u
            arrived = ngot[t - (groups - near) * size].astype(jnp.float32)
            xout[mine, t] = (xout[mine, t].astype(jnp.float32) + arrived).astype(half)
        for u in range(turns // groups):
            y_copy(g * (turns // groups) + u).start()

    @pl.when(edge)
    def _():
        with jax.named_scope("edge_first"):
            loop(0, groups, lambda g: forward(0, g, False))
            loop(groups - near, groups, merge)
        with jax.named_scope("edge_middle"):
            over_planes(1, planes - 2, lambda i: loop(0, groups, lambda g: forward(i, g, False)))
        with jax.named_scope("edge_last"):
            loop(0, groups - near, lambda g: forward(planes - 2, g, False))
            loop(groups - near, groups, lambda g: forward(planes - 2, g, False, crossed=False))

    @pl.when(jnp.logical_not(edge))
    def _():
        with jax.named_scope("inner_first"):
            loop(0, groups, lambda g: forward(0, g, True))
            loop(groups - near, groups, merge)

        def both(g):
            forward(planes - 3, g, True)
            forward(planes - 2, g + groups - near, True, crossed=False)

        def rest(g):
            forward(planes - 3, g, True)
            forward(planes - 2, g - near, True)
        with jax.named_scope("inner_middle"):
            over_planes(1, planes - 3, lambda i: loop(0, groups, lambda g: forward(i, g, True)))
        with jax.named_scope("inner_both"):
            loop(0, near, both)
            loop(near, groups, rest)

    small[3].wait()

    def finish(j):
        with jax.named_scope("finish_x"):
            y_copy(j).wait_recv()
        if j % (turns // groups) == 0:
            g = j // (turns // groups)
            with jax.named_scope("finish_z"):
                pl.when(mine > 0)(lambda: z_wait(mine, g))
                pl.when(mine < planes - 1)(lambda: z_wait(planes, g))
        found = []
        for u in range(step):
            t = j * step + u
            total = cell(mine, t) + xgot[mine, t].astype(jnp.float32)
            total = total + zgot[mine, t].astype(jnp.float32) + zgot[planes, t].astype(jnp.float32)
            found.append(total.astype(jnp.bfloat16))
        done = jnp.dot(jnp.concatenate(found, axis=0), kern_v[...], preferred_element_type=jnp.float32)
        for u in range(step):
            out[:, j * step + u, :] = done[u * share:(u + 1) * share]

    with jax.named_scope("leave"):
        swap.wait_send()
        pltpu.make_async_remote_copy(
            src_ref=dout, dst_ref=dgot, send_sem=dsend, recv_sem=srecv, device_id=pair, device_id_type=MESH,
        ).wait_send()

    for j in range(turns):
        with jax.named_scope("finish"):
            finish(j)
    with jax.named_scope("leave"):
        pltpu.make_async_remote_copy(
            src_ref=xout, dst_ref=xgot, send_sem=xsend, recv_sem=srecv, device_id=across, device_id_type=MESH,
        ).wait_send()
        pltpu.make_async_remote_copy(
            src_ref=xgot.at[0:planes - 1], dst_ref=zgot.at[0:planes - 1], send_sem=zsend, recv_sem=srecv,
            device_id=beside, device_id_type=MESH,
        ).wait_send()


def exchange(bins, spots, vis, rows, cols, kern, planes, tiles):
    count, fold, _, share, width = rows.shape
    wide = 2 * cols.shape[2]
    groups, turns = PARTS, TURNS
    near = NEAR if planes <= 4 else 0
    size = tiles // groups
    any_spec = pl.BlockSpec(memory_space=pltpu.HBM)
    half = jnp.bfloat16
    dma = pltpu.SemaphoreType.DMA
    table = (-(-(1 + -(-planes * tiles // 128)) // 8) * 8, 128)
    grids = (2 * planes + planes + 1 + 2) * tiles * share * wide * 2
    held = 2 * (rows.size + cols.size + kern.size) + 8 * (count + 1) * share * wide + 8 * count * share * wide
    limit = min(LIMIT, grids + held + 6 * 1024 * 1024)
    operands = [pltpu.with_memory_space_constraint(a, pltpu.HBM) for a in (bins, spots, vis, rows, cols, kern)]
    return pl.pallas_call(
        functools.partial(exchange_kernel, planes, tiles, groups, turns, near),
        out_shape=jax.ShapeDtypeStruct((share, tiles, wide), jnp.float32),
        in_specs=[any_spec] * 6,
        out_specs=pl.BlockSpec(memory_space=pltpu.VMEM),
        scratch_shapes=[
            pltpu.VMEM(bins.shape, jnp.int32),
            pltpu.VMEM(spots.shape, jnp.int32),
            pltpu.SMEM((2,) + table, jnp.int32),
            pltpu.VMEM((2,) + table, jnp.int32),
            pltpu.VMEM(vis.shape, vis.dtype),
            pltpu.VMEM(rows.shape, rows.dtype),
            pltpu.VMEM(cols.shape, cols.dtype),
            pltpu.VMEM(kern.shape, kern.dtype),
            pltpu.VMEM((2, count + 1, share, wide), jnp.float32),
            pltpu.VMEM((2, count, 2 * share, wide // 2), half),
            pltpu.VMEM((2, count, 2 * share, wide // 2), half),
            pltpu.VMEM((planes, tiles, share, wide), half),
            pltpu.VMEM((planes, tiles, share, wide), half),
            pltpu.VMEM((planes + 1, tiles, share, wide), half),
            pltpu.VMEM((max(near, 1) * size, share, wide), half),
            dma((6,)),
            dma((2, PIECES)),
            dma,
            dma,
            dma,
            dma((2, PIECES)),
            dma,
            dma((planes - 1, groups)),
            dma((turns,)),
            dma,
            dma((planes + 1, groups)),
            dma((max(near, 1),)),
        ],
        compiler_params=pltpu.CompilerParams(
            collective_id=0, has_side_effects=True, vmem_limit_bytes=limit
        ),
        name="exchange",
    )(*operands)


def body(vis, row_weight, col_weight, w_bin, tile_col, w_kernel):
    planes = lax.axis_size("tm")
    chans = lax.axis_size("chan")
    count, rows_k, width_v = row_weight.shape[1:]
    tile_count = GC // QW
    fold = chans // 2
    bins = w_bin.reshape(1, count)
    rows = row_weight[0].reshape(count, fold, 2, rows_k // chans, width_v)
    result = exchange(bins, tile_col, vis[0], rows, col_weight[0], w_kernel[0], planes, tile_count)
    return result[None]


def solution(mesh):
    in_specs = (
        P(("groups", "chan"), "tm", None, None),
        P(("groups", "chan"), "tm", None, None),
        P(("groups", "chan"), "tm", None, None),
        P(("groups", "chan"), "tm", None),
        P(("groups", "chan"), "tm"),
        P(("groups", "tm"), None, None),
    )
    out_specs = P(("groups", "tm"), "chan", None, None)
    return jax.shard_map(body, mesh=mesh, in_specs=in_specs, out_specs=out_specs, check_vma=False)
```

time: 61.3 us -> 49.9 us (0.81)
  Pallas kernels: 60.2 us -> 48.7 us
    pallas_call x1, Pallas kernels: 60.2 us -> 48.7 us  [exchange(): pl.pallas_call(functools.partial(exchange_kernel, planes, tiles, groups,...]
where the time goes in v3:
time: 49.9 us; the launch traced here: 49.7 us
  Pallas kernels  48.7 us (98%)
  local copies, waits for them, and re-layouts  0.97 us (2%)
    pallas_call x1, Pallas kernels, exchange(): pl.pallas_call(functools.partial(exchange_kernel, planes, tiles, groups,...  48.7 us

profile of v3, /device:TPU:0, one launch (start us, length us, event | category | flops | bytes accessed | tf_op | source)
XLA Modules:
  0.0 49.7 jit_solution(6713553304177653478)
XLA Ops:
  0.0 48.7 %exchange.1 = f32[32,16,512]{2,1,0:T(8,128)S(1)} custom-call(s32[1,32]{1,0:T(1,128)} %bitcast.11, s32[1,32]{1,0:T(1,128)} %spots.1, bf16[32,2,128]{2,1,0:T(2,128)(2,1)} %bitcast.10, bf16[32,2,2,32,128]{4,3,2,1,0:T(8,128)(2,1)} %bitcast.8, bf16[32,128,256]{2,1,0:T(8,128)(2,1)} %bitcast.7, bf16[512,512]{1,0:T(8,128)(2,1)} %bitcast.9), custom_call_target="tpu_custom_call" | custom-call | tf_op jit(solution)/shard_map/exchange/pallas_call | solution.py:372
  48.7 1.0 %copy.8 = f32[1,32,16,512]{3,2,1,0:T(8,128)} copy(f32[1,32,16,512]{3,2,1,0:T(8,128)S(1)} %bitcast.6) | data formatting | bytes 2097152

commit v4 on v3

v4 whole, which is shorter than its diff:
```python
import functools
import jax
import jax.numpy as jnp
from jax import lax
from jax.experimental import pallas as pl
from jax.experimental.pallas import tpu as pltpu
from jax.sharding import PartitionSpec as P

QW = 256
GC = 4096
MESH = pl.DeviceIdType.MESH
LIMIT = 63 * 1024 * 1024
PIECES = 4
NEAR = 9


def write_table(table, bins, spots, cells, tiles):
    count = bins.shape[1]
    down = lax.broadcasted_iota(jnp.int32, (count, count), 0)
    along = lax.broadcasted_iota(jnp.int32, (count, count), 1)
    flat = jnp.broadcast_to(bins * tiles + spots, (count, count))
    tall = jnp.max(jnp.where(down == along, flat, 0), axis=1, keepdims=True)
    before = jnp.max(jnp.where((tall == flat) & (down < along), down + 1, 0), axis=0, keepdims=True)
    table[...] = jnp.zeros(table.shape, jnp.int32)
    table[0:1, 0:count] = before
    deep = lax.broadcasted_iota(jnp.int32, (count, 128), 0)
    wide = lax.broadcasted_iota(jnp.int32, (count, 128), 1)
    for r in range(-(-cells // 128)):
        named = tall == wide + r * 128
        table[1 + r:2 + r, :] = jnp.max(jnp.where(named, deep + 1, 0), axis=0, keepdims=True)


def loop(start, stop, step):
    def body(i, carry):
        step(i)
        return carry
    lax.fori_loop(start, stop, body, 0)


def messages(planes, tiles, share):
    quarter, half = tiles // 4, share // 2
    even = [(q * quarter, quarter, 0, share) for q in range(4)]
    if planes != 4:
        own = [(t, 2) for t in range(0, tiles, 2)]
        return [even] * (planes - 1), [], own, tiles
    split = tiles - NEAR
    first = [(t, tiles // 2, r, half) for r in (0, half) for t in (tiles // 2, 0)]
    last = [(0, quarter, 0, share), (quarter, split - quarter, 0, share)]
    middle = split + (NEAR + 1) // 2
    last += [(split, middle - split, 0, share), (middle, tiles - middle, 0, share)]
    near = [(split, NEAR, r, half) for r in (0, half)]
    own = [(t, min(2, split - t)) for t in range(0, split, 2)]
    own += [(t, min(2, tiles - t)) for t in range(split, tiles, 2)]
    return [first, even, last], near, own, split


def exchange_kernel(
    planes, tiles, bins, spots, vis, rows, cols, kern, out,
    bins_v, spots_v, tab_s, tab_v, vis_v, rows_v, cols_v, kern_v, runs, dout, dgot, xout, xgot, zgot, ngot,
    lsem, psem, ssend, srecv, dsend, drecv, xsend, xrecv, yrecv, zsend, zrecv, nrecv,
):
    me, mine = lax.axis_index("chan"), lax.axis_index("tm")
    core, row = me % 2, me // 2
    pair = {"chan": row * 2 + 1 - core}
    across = {"chan": (1 - row) * 2 + core}
    count, share = rows_v.shape[0], rows_v.shape[3]
    half_rows = share // 2
    piece = count // PIECES
    narrow = xout.dtype
    edge = mine % (planes - 1) == 0
    up = mine // (planes // 2)
    reach = up * mine + (1 - up) * (planes - 1 - mine)
    beside = {"tm": mine + 1 - 2 * (mine % 2)}
    lists, near, own_list, split = messages(planes, tiles, share)
    short = len(near) > 0

    def less(a, b):
        return (planes - 1 + b - a) // planes

    def plane(i):
        late = i // reach
        v = (1 - late) * i + late * (planes - 1 - (i - reach))
        return up * v + (1 - up) * (planes - 1 - v)

    def slot(w):
        return w + less(w, mine) * (1 - less(w, mine - 1)) * (planes - w)

    def list_of(i):
        return lists[i] if short else lists[0]

    small = [
        pltpu.make_async_copy(src, dst, lsem.at[i])
        for i, (src, dst) in enumerate(((bins, bins_v), (spots, spots_v), (vis, vis_v), (kern, kern_v)))
    ]
    parts = []
    for p in range(PIECES):
        cut = pl.ds(p * piece, piece)
        parts.append([
            pltpu.make_async_copy(rows.at[cut], rows_v.at[cut], psem.at[0, p]),
            pltpu.make_async_copy(cols.at[cut], cols_v.at[cut], psem.at[1, p]),
        ])
    for copy in small[:3] + sum(parts, []) + small[3:]:
        copy.start()

    barrier = pltpu.get_barrier_semaphore()
    pl.semaphore_signal(barrier, inc=1, device_id=pair, device_id_type=MESH)
    pl.semaphore_signal(barrier, inc=1, device_id=across, device_id_type=MESH)

    def greet(step):
        pl.semaphore_signal(barrier, inc=1, device_id={"tm": mine + step}, device_id_type=MESH)
    pl.when(mine > 0)(lambda: greet(-1))
    pl.when(mine < planes - 1)(lambda: greet(1))

    tables = [pltpu.make_async_copy(tab_v.at[i], tab_s.at[i], lsem.at[4 + i]) for i in range(2)]
    swap = pltpu.make_async_remote_copy(
        src_ref=tab_v.at[0], dst_ref=tab_v.at[1], send_sem=ssend, recv_sem=srecv, device_id=pair, device_id_type=MESH,
    )
    for s in range(2):
        runs[s, 0] = jnp.zeros(runs.shape[2:], runs.dtype)

    @pl.when(edge)
    def _():
        zgot[(mine // (planes - 1)) * planes] = jnp.zeros(zgot.shape[1:], narrow)

    def entry(s, i):
        return tab_s[s, i // 128, i % 128]

    def d_copy(r, p):
        cut = pl.ds(p * (count // 2), count // 2)
        return pltpu.make_async_remote_copy(
            src_ref=dout.at[0, r, cut], dst_ref=dgot.at[0, r, cut], send_sem=dsend, recv_sem=drecv.at[2 * r + p],
            device_id=pair, device_id_type=MESH,
        )

    def e_copy(p):
        cut = pl.ds(p * (count // 2), count // 2)
        return pltpu.make_async_remote_copy(
            src_ref=dout.at[1, :, cut], dst_ref=dgot.at[1, :, cut], send_sem=dsend, recv_sem=drecv.at[4 + p],
            device_id=pair, device_id_type=MESH,
        )

    def build_other(s, x, p):
        for b in range(p * piece, (p + 1) * piece):
            other = rows_v[b, x, 1 - core]
            real, imag = vis_v[b, 0:1, :], vis_v[b, 1:2, :]
            upper, lower = other[:half_rows], other[half_rows:]
            weighted = jnp.concatenate([upper * real, upper * imag, lower * real, lower * imag], axis=0)
            found = jnp.dot(weighted, cols_v[b], preferred_element_type=jnp.float32).astype(narrow)
            dout[s, 0, b] = found[:share]
            dout[s, 1, b] = found[share:]

    def build_own(x, p):
        for b in range(p * piece, (p + 1) * piece):
            own = rows_v[b, x, core]
            real, imag = vis_v[b, 0:1, :], vis_v[b, 1:2, :]
            weighted = jnp.concatenate([own * real, own * imag], axis=0)
            found = jnp.dot(weighted, cols_v[b], preferred_element_type=jnp.float32)
            runs[0, b + 1, :, 0:QW] = found[:share]
            runs[0, b + 1, :, QW:2 * QW] = found[share:]

    batch = 4 if count % 8 == 0 else 1

    def chain(low, high):
        def step(i):
            for u in range(batch):
                b = i * batch + u
                runs[0, b + 1, low:high] = runs[0, b + 1, low:high] + runs[0, entry(0, b), low:high]
        loop(0, count // batch, step)

    def join(s, r, p):
        low, high = r * half_rows, (r + 1) * half_rows

        def step(i):
            for u in range(batch):
                b = p * (count // 2) + i * batch + u
                found, last = dgot[s, r, b].astype(jnp.float32), entry(1, b)
                runs[1, b + 1, low:high, 0:QW] = found[:half_rows] + runs[1, last, low:high, 0:QW]
                runs[1, b + 1, low:high, QW:2 * QW] = found[half_rows:] + runs[1, last, low:high, QW:2 * QW]
        loop(0, count // 2 // batch, step)

    def cell(w, t, low, high):
        i = 128 + w * tiles + t
        return runs[0, entry(0, i), low:high] + runs[1, entry(1, i), low:high]

    def window(ref, w, m):
        start, many, low, deep = m
        return ref.at[w, start:start + many, low:low + deep]

    def x_copy(i, n):
        w, m = plane(i), list_of(i)[n]
        return pltpu.make_async_remote_copy(
            src_ref=window(xout, w, m), dst_ref=window(xgot, w, m),
            send_sem=xsend, recv_sem=xrecv.at[i, n], device_id=across, device_id_type=MESH,
        )

    def y_copy(n):
        m = own_list[n] + (0, share)
        return pltpu.make_async_remote_copy(
            src_ref=window(xout, mine, m), dst_ref=window(xgot, mine, m),
            send_sem=xsend, recv_sem=yrecv.at[n], device_id=across, device_id_type=MESH,
        )

    def z_copy(i, n):
        w, m = plane(i), list_of(i)[n]
        return pltpu.make_async_remote_copy(
            src_ref=window(xgot, w, m), dst_ref=window(zgot, slot(w), m),
            send_sem=zsend, recv_sem=zrecv.at[slot(w), n],
            device_id={"tm": mine + 2 * less(mine, w) - 1}, device_id_type=MESH,
        )

    def z_wait(at, m, n):
        pltpu.make_async_remote_copy(
            src_ref=window(xgot, 0, m), dst_ref=window(zgot, at, m),
            send_sem=zsend, recv_sem=zrecv.at[at, n], device_id=beside, device_id_type=MESH,
        ).wait_recv()

    def near_copy(n):
        start, many, low, deep = near[n]
        return pltpu.make_async_remote_copy(
            src_ref=window(xout, plane(planes - 2), near[n]), dst_ref=ngot.at[:, low:low + deep],
            send_sem=xsend, recv_sem=nrecv.at[n], device_id=beside, device_id_type=MESH,
        )

    def over_tiles(start, many, step):
        pairs = many // 2

        def two(i):
            step(start + 2 * i)
            step(start + 2 * i + 1)
        loop(0, pairs, two)
        if many % 2:
            step(start + many - 1)

    def fill(w, m):
        start, many, low, deep = m

        def step(t):
            xout[w, t, low:low + deep] = cell(w, t, low, low + deep).astype(narrow)
        over_tiles(start, many, step)

    def send(i, n):
        fill(plane(i), list_of(i)[n])
        x_copy(i, n).start()

    def approach(n):
        fill(plane(planes - 2), near[n])
        near_copy(n).start()

    with jax.named_scope("table"):
        for copy in small[:2]:
            copy.wait()
        write_table(tab_v.at[0], bins_v[...], spots_v[...], planes * tiles, tiles)
        tables[0].start()
    with jax.named_scope("vis_wait"):
        small[2].wait()
    for p in range(PIECES):
        with jax.named_scope("load_wait"):
            for copy in parts[p]:
                copy.wait()
        with jax.named_scope("build_other"):
            build_other(0, 1 - row, p)
        if p == PIECES // 2 - 1:
            with jax.named_scope("barrier"):
                pl.semaphore_wait(barrier, 3 + less(0, mine) * less(mine, planes - 1))
            swap.start()
            d_copy(0, 0).start()
    d_copy(0, 1).start()
    d_copy(1, 0).start()
    d_copy(1, 1).start()
    for p in range(PIECES):
        with jax.named_scope("build_own"):
            build_own(1 - row, p)
    with jax.named_scope("swap_wait"):
        swap.wait_recv()
        tables[1].start()
        tables[0].wait()
    with jax.named_scope("chain_far"):
        chain(0, half_rows)
        chain(half_rows, share)
    with jax.named_scope("table_wait"):
        tables[1].wait()
    for p in range(2):
        with jax.named_scope("pair_wait"):
            d_copy(0, p).wait_recv()
        with jax.named_scope("join_far"):
            join(0, 0, p)
    if short:
        with jax.named_scope("fill_first"):
            send(0, 0)
            approach(0)
            send(0, 1)
    for p in range(2):
        with jax.named_scope("pair_wait"):
            d_copy(1, p).wait_recv()
        with jax.named_scope("join_far"):
            join(0, 1, p)
    with jax.named_scope("fill"):
        if short:
            send(0, 2)
            send(0, 3)
            approach(1)
            for n in range(len(lists[1])):
                send(1, n)
            for n in range(2):
                send(2, n)
        else:
            def send_all(i):
                for n in range(len(list_of(i))):
                    send(i, n)
            loop(0, planes - 1, send_all)
        for n, m in enumerate(own_list):
            fill(mine, m + (0, share))
            if m[0] < split:
                y_copy(n).start()

    for p in range(PIECES):
        with jax.named_scope("build_near"):
            build_other(1, row, p)
        if p % 2:
            e_copy(p // (PIECES // 2)).start()
    for p in range(PIECES):
        with jax.named_scope("build_near"):
            build_own(row, p)
    with jax.named_scope("chain_near"):
        chain(0, share)
    for p in range(2):
        with jax.named_scope("join_near"):
            e_copy(p).wait_recv()
            join(1, 0, p)
            join(1, 1, p)

    def gather(w, m, crossed, joined):
        start, many, low, deep = m
        high = low + deep

        def step(t):
            total = cell(w, t, low, high)
            if crossed:
                total = total + xgot[w, t, low:high].astype(jnp.float32)
            if joined:
                total = total + zgot[w, t, low:high].astype(jnp.float32)
            xgot[w, t, low:high] = total.astype(narrow)
        over_tiles(start, many, step)

    def forward(i, n, joined, crossed=True, wait=True):
        w, m = plane(i), list_of(i)[n]
        if crossed:
            x_copy(i, n).wait_recv()
        if joined and wait:
            z_wait(w, m, n)
        gather(w, m, crossed, joined)
        z_copy(i, n).start()

    def merge():
        for n in range(len(near)):
            near_copy(n).wait_recv()

        def step(t):
            arrived = ngot[t - split].astype(jnp.float32)
            xout[mine, t] = (xout[mine, t].astype(jnp.float32) + arrived).astype(narrow)
        for n, m in enumerate(own_list):
            if m[0] >= split:
                over_tiles(m[0], m[1], step)
                y_copy(n).start()

    def forward_all(i, joined):
        for n in range(len(list_of(i))):
            forward(i, n, joined)

    @pl.when(edge)
    def _():
        if short:
            with jax.named_scope("edge_first"):
                forward_all(0, False)
                merge()
            with jax.named_scope("edge_middle"):
                forward_all(1, False)
            with jax.named_scope("edge_last"):
                for n in range(len(lists[2])):
                    forward(2, n, False, crossed=n < 2)
        else:
            loop(0, planes - 1, lambda i: forward_all(i, False))

    @pl.when(jnp.logical_not(edge))
    def _():
        if short:
            with jax.named_scope("inner_first"):
                forward_all(0, True)
                merge()
            with jax.named_scope("inner_both"):
                forward(1, 0, True)
                for n, m in enumerate(lists[0]):
                    z_wait(plane(2), m, n)
                forward(2, 2, True, crossed=False, wait=False)
                forward(1, 1, True)
                forward(2, 3, True, crossed=False, wait=False)
                forward(1, 2, True)
                forward(2, 0, True, wait=False)
                forward(1, 3, True)
                forward(2, 1, True, wait=False)
        else:
            loop(0, planes - 1, lambda i: forward_all(i, True))

    small[3].wait()
    swap.wait_send()
    pltpu.make_async_remote_copy(
        src_ref=dout, dst_ref=dgot, send_sem=dsend, recv_sem=srecv, device_id=pair, device_id_type=MESH,
    ).wait_send()

    held = {False: 0, True: 0}

    def arrive(stop):
        beyond = mine + (1 - mine % 2) * (planes - mine)
        for far, group in ((False, lists[-1]), (True, lists[-2])):
            at = mine + planes - beyond if far else beyond
            done = sorted(range(len(group)), key=lambda n: group[n][0])
            while held[far] < len(done) and group[done[held[far]]][0] < stop:
                n = done[held[far]]
                held[far] += 1
                if far:
                    pl.when(jnp.logical_not(edge))(functools.partial(z_wait, at, group[n], n))
                elif short:
                    z_wait(at, group[n], n)
                else:
                    pl.when(jnp.logical_or(jnp.logical_not(edge), beyond == planes * (1 - up) + mine * up))(
                        functools.partial(z_wait, at, group[n], n))

    for n, (start, many) in enumerate(own_list):
        with jax.named_scope("finish_x"):
            y_copy(n).wait_recv()
        with jax.named_scope("finish_z"):
            arrive(start + many)
        with jax.named_scope("finish"):
            found = []
            for t in range(start, start + many):
                total = cell(mine, t, 0, share) + xgot[mine, t].astype(jnp.float32)
                total = total + zgot[mine, t].astype(jnp.float32) + zgot[planes, t].astype(jnp.float32)
                found.append(total.astype(jnp.bfloat16))
            done = jnp.dot(jnp.concatenate(found, axis=0), kern_v[...], preferred_element_type=jnp.float32)
            for u in range(many):
                out[:, start + u, :] = done[u * share:(u + 1) * share]
    with jax.named_scope("leave"):
        pltpu.make_async_remote_copy(
            src_ref=xout, dst_ref=xgot, send_sem=xsend, recv_sem=srecv, device_id=across, device_id_type=MESH,
        ).wait_send()
        pltpu.make_async_remote_copy(
            src_ref=xgot.at[0:planes - 1], dst_ref=zgot.at[0:planes - 1], send_sem=zsend, recv_sem=srecv,
            device_id=beside, device_id_type=MESH,
        ).wait_send()


def exchange(bins, spots, vis, rows, cols, kern, planes, tiles):
    count, fold, _, share, width = rows.shape
    wide = 2 * cols.shape[2]
    lists, near, own_list, split = messages(planes, tiles, share)
    any_spec = pl.BlockSpec(memory_space=pltpu.HBM)
    half = jnp.bfloat16
    dma = pltpu.SemaphoreType.DMA
    table = (-(-(1 + -(-planes * tiles // 128)) // 8) * 8, 128)
    grids = (2 * planes + planes + 1 + 2) * tiles * share * wide * 2
    held = 2 * (rows.size + cols.size + kern.size) + 8 * (count + 1) * share * wide + 8 * count * share * wide
    limit = min(LIMIT, grids + held + 6 * 1024 * 1024)
    operands = [pltpu.with_memory_space_constraint(a, pltpu.HBM) for a in (bins, spots, vis, rows, cols, kern)]
    return pl.pallas_call(
        functools.partial(exchange_kernel, planes, tiles),
        out_shape=jax.ShapeDtypeStruct((share, tiles, wide), jnp.float32),
        in_specs=[any_spec] * 6,
        out_specs=pl.BlockSpec(memory_space=pltpu.VMEM),
        scratch_shapes=[
            pltpu.VMEM(bins.shape, jnp.int32),
            pltpu.VMEM(spots.shape, jnp.int32),
            pltpu.SMEM((2,) + table, jnp.int32),
            pltpu.VMEM((2,) + table, jnp.int32),
            pltpu.VMEM(vis.shape, vis.dtype),
            pltpu.VMEM(rows.shape, rows.dtype),
            pltpu.VMEM(cols.shape, cols.dtype),
            pltpu.VMEM(kern.shape, kern.dtype),
            pltpu.VMEM((2, count + 1, share, wide), jnp.float32),
            pltpu.VMEM((2, 2, count, share, wide // 2), half),
            pltpu.VMEM((2, 2, count, share, wide // 2), half),
            pltpu.VMEM((planes, tiles, share, wide), half),
            pltpu.VMEM((planes, tiles, share, wide), half),
            pltpu.VMEM((planes + 1, tiles, share, wide), half),
            pltpu.VMEM((max(tiles - split, 1), share, wide), half),
            dma((6,)),
            dma((2, PIECES)),
            dma,
            dma,
            dma,
            dma((6,)),
            dma,
            dma((planes - 1, 4)),
            dma((len(own_list),)),
            dma,
            dma((planes + 1, 4)),
            dma((2,)),
        ],
        compiler_params=pltpu.CompilerParams(
            collective_id=0, has_side_effects=True, vmem_limit_bytes=limit
        ),
        name="exchange",
    )(*operands)


def body(vis, row_weight, col_weight, w_bin, tile_col, w_kernel):
    planes = lax.axis_size("tm")
    chans = lax.axis_size("chan")
    count, rows_k, width_v = row_weight.shape[1:]
    tile_count = GC // QW
    fold = chans // 2
    bins = w_bin.reshape(1, count)
    rows = row_weight[0].reshape(count, fold, 2, rows_k // chans, width_v)
    result = exchange(bins, tile_col, vis[0], rows, col_weight[0], w_kernel[0], planes, tile_count)
    return result[None]


def solution(mesh):
    in_specs = (
        P(("groups", "chan"), "tm", None, None),
        P(("groups", "chan"), "tm", None, None),
        P(("groups", "chan"), "tm", None, None),
        P(("groups", "chan"), "tm", None),
        P(("groups", "chan"), "tm"),
        P(("groups", "tm"), None, None),
    )
    out_specs = P(("groups", "tm"), "chan", None, None)
    return jax.shard_map(body, mesh=mesh, in_specs=in_specs, out_specs=out_specs, check_vma=False)
```

time: 49.9 us -> 49.2 us (0.986); the launches traced: 49.7 us -> 48.4 us
  Pallas kernels: 48.7 us -> 47.5 us
    pallas_call x1, Pallas kernels: 48.7 us -> 47.5 us  [exchange(): pl.pallas_call(functools.partial(exchange_kernel, planes, tiles), out_sha...]
where the time goes in v4:
time: 49.2 us; the launch traced here: 48.4 us
  Pallas kernels  47.5 us (97%)
  local copies, waits for them, and re-layouts  0.97 us (2%)
    pallas_call x1, Pallas kernels, exchange(): pl.pallas_call(functools.partial(exchange_kernel, planes, tiles), out_sha...  47.5 us

profile of v4, /device:TPU:0, one launch (start us, length us, event | category | flops | bytes accessed | tf_op | source)
XLA Modules:
  0.0 48.4 jit_solution(8690167686264613234)
XLA Ops:
  0.0 47.5 %exchange.1 = f32[32,16,512]{2,1,0:T(8,128)S(1)} custom-call(s32[1,32]{1,0:T(1,128)} %bitcast.11, s32[1,32]{1,0:T(1,128)} %spots.1, bf16[32,2,128]{2,1,0:T(2,128)(2,1)} %bitcast.10, bf16[32,2,2,32,128]{4,3,2,1,0:T(8,128)(2,1)} %bitcast.8, bf16[32,128,256]{2,1,0:T(8,128)(2,1)} %bitcast.7, bf16[512,512]{1,0:T(8,128)(2,1)} %bitcast.9), custom_call_target="tpu_custom_call" | custom-call | tf_op jit(solution)/shard_map/exchange/pallas_call | solution.py:464
  47.5 1.0 %copy.8 = f32[1,32,16,512]{3,2,1,0:T(8,128)} copy(f32[1,32,16,512]{3,2,1,0:T(8,128)S(1)} %bitcast.6) | data formatting | bytes 2097152

commit v5 on v4

--- a/solution.py
+++ b/solution.py
@@ -10,7 +10,7 @@
 GC = 4096
 MESH = pl.DeviceIdType.MESH
 LIMIT = 63 * 1024 * 1024
-PIECES = 4
+PIECES = 2
 NEAR = 9
 
 
@@ -46,17 +46,18 @@
     split = tiles - NEAR
     first = [(t, tiles // 2, r, half) for r in (0, half) for t in (tiles // 2, 0)]
     last = [(0, quarter, 0, share), (quarter, split - quarter, 0, share)]
-    middle = split + (NEAR + 1) // 2
-    last += [(split, middle - split, 0, share), (middle, tiles - middle, 0, share)]
+    last += [(split, NEAR - 2, 0, share), (tiles - 2, 2, 0, share)]
     near = [(split, NEAR, r, half) for r in (0, half)]
     own = [(t, min(2, split - t)) for t in range(0, split, 2)]
-    own += [(t, min(2, tiles - t)) for t in range(split, tiles, 2)]
+    own += [(t, 2) for t in range(split, tiles - 5, 2)]
+    at = own[-1][0] + own[-1][1]
+    own += [(at, tiles - 2 - at), (tiles - 2, 2)]
     return [first, even, last], near, own, split
 
 
 def exchange_kernel(
     planes, tiles, bins, spots, vis, rows, cols, kern, out,
-    bins_v, spots_v, tab_s, tab_v, vis_v, rows_v, cols_v, kern_v, runs, dout, dgot, xout, xgot, zgot, ngot,
+    bins_v, spots_v, tab_s, tab_v, vis_v, rows_v, cols_v, kern_v, runs, pairs, dout, dgot, xout, xgot, zgot, ngot,
     lsem, psem, ssend, srecv, dsend, drecv, xsend, xrecv, yrecv, zsend, zrecv, nrecv,
 ):
     me, mine = lax.axis_index("chan"), lax.axis_index("tm")
@@ -111,12 +112,12 @@
     pl.when(mine > 0)(lambda: greet(-1))
     pl.when(mine < planes - 1)(lambda: greet(1))
 
-    tables = [pltpu.make_async_copy(tab_v.at[i], tab_s.at[i], lsem.at[4 + i]) for i in range(2)]
+    table = pltpu.make_async_copy(tab_v, tab_s.at[0], lsem.at[4])
     swap = pltpu.make_async_remote_copy(
-        src_ref=tab_v.at[0], dst_ref=tab_v.at[1], send_sem=ssend, recv_sem=srecv, device_id=pair, device_id_type=MESH,
+        src_ref=tab_v, dst_ref=tab_s.at[1], send_sem=ssend, recv_sem=srecv, device_id=pair, device_id_type=MESH,
     )
-    for s in range(2):
-        runs[s, 0] = jnp.zeros(runs.shape[2:], runs.dtype)
+    runs[0] = jnp.zeros(runs.shape[1:], runs.dtype)
+    pairs[0] = jnp.zeros(pairs.shape[1:], pairs.dtype)
 
     @pl.when(edge)
     def _():
@@ -155,17 +156,10 @@
             real, imag = vis_v[b, 0:1, :], vis_v[b, 1:2, :]
             weighted = jnp.concatenate([own * real, own * imag], axis=0)
             found = jnp.dot(weighted, cols_v[b], preferred_element_type=jnp.float32)
-            runs[0, b + 1, :, 0:QW] = found[:share]
-            runs[0, b + 1, :, QW:2 * QW] = found[share:]
+            runs[b + 1, :, 0:QW] = found[:share]
+            runs[b + 1, :, QW:2 * QW] = found[share:]
 
     batch = 4 if count % 8 == 0 else 1
-
-    def chain(low, high):
-        def step(i):
-            for u in range(batch):
-                b = i * batch + u
-                runs[0, b + 1, low:high] = runs[0, b + 1, low:high] + runs[0, entry(0, b), low:high]
-        loop(0, count // batch, step)
 
     def join(s, r, p):
         low, high = r * half_rows, (r + 1) * half_rows
@@ -173,14 +167,15 @@
         def step(i):
             for u in range(batch):
                 b = p * (count // 2) + i * batch + u
-                found, last = dgot[s, r, b].astype(jnp.float32), entry(1, b)
-                runs[1, b + 1, low:high, 0:QW] = found[:half_rows] + runs[1, last, low:high, 0:QW]
-                runs[1, b + 1, low:high, QW:2 * QW] = found[half_rows:] + runs[1, last, low:high, QW:2 * QW]
+                found, own, last = dgot[s, r, b].astype(jnp.float32), entry(0, b), entry(1, b)
+                runs[b + 1, low:high] = runs[b + 1, low:high] + runs[own, low:high]
+                pairs[b + 1, low:high, 0:QW] = found[:half_rows] + pairs[last, low:high, 0:QW]
+                pairs[b + 1, low:high, QW:2 * QW] = found[half_rows:] + pairs[last, low:high, QW:2 * QW]
         loop(0, count // 2 // batch, step)
 
     def cell(w, t, low, high):
         i = 128 + w * tiles + t
-        return runs[0, entry(0, i), low:high] + runs[1, entry(1, i), low:high]
+        return runs[entry(0, i), low:high] + pairs[entry(1, i), low:high]
 
     def window(ref, w, m):
         start, many, low, deep = m
@@ -249,8 +244,8 @@
     with jax.named_scope("table"):
         for copy in small[:2]:
             copy.wait()
-        write_table(tab_v.at[0], bins_v[...], spots_v[...], planes * tiles, tiles)
-        tables[0].start()
+        write_table(tab_v, bins_v[...], spots_v[...], planes * tiles, tiles)
+        table.start()
     with jax.named_scope("vis_wait"):
         small[2].wait()
     for p in range(PIECES):
@@ -259,26 +254,19 @@
                 copy.wait()
         with jax.named_scope("build_other"):
             build_other(0, 1 - row, p)
-        if p == PIECES // 2 - 1:
+        if p == 0:
             with jax.named_scope("barrier"):
                 pl.semaphore_wait(barrier, 3 + less(0, mine) * less(mine, planes - 1))
             swap.start()
-            d_copy(0, 0).start()
-    d_copy(0, 1).start()
-    d_copy(1, 0).start()
-    d_copy(1, 1).start()
+        d_copy(0, p).start()
+    for p in range(PIECES):
+        d_copy(1, p).start()
     for p in range(PIECES):
         with jax.named_scope("build_own"):
             build_own(1 - row, p)
     with jax.named_scope("swap_wait"):
         swap.wait_recv()
-        tables[1].start()
-        tables[0].wait()
-    with jax.named_scope("chain_far"):
-        chain(0, half_rows)
-        chain(half_rows, share)
-    with jax.named_scope("table_wait"):
-        tables[1].wait()
+        table.wait()
     for p in range(2):
         with jax.named_scope("pair_wait"):
             d_copy(0, p).wait_recv()
@@ -316,13 +304,10 @@
     for p in range(PIECES):
         with jax.named_scope("build_near"):
             build_other(1, row, p)
-        if p % 2:
-            e_copy(p // (PIECES // 2)).start()
+        e_copy(p).start()
     for p in range(PIECES):
         with jax.named_scope("build_near"):
             build_own(row, p)
-    with jax.named_scope("chain_near"):
-        chain(0, share)
     for p in range(2):
         with jax.named_scope("join_near"):
             e_copy(p).wait_recv()
@@ -470,19 +455,20 @@
             pltpu.VMEM(bins.shape, jnp.int32),
             pltpu.VMEM(spots.shape, jnp.int32),
             pltpu.SMEM((2,) + table, jnp.int32),
-            pltpu.VMEM((2,) + table, jnp.int32),
+            pltpu.VMEM(table, jnp.int32),
             pltpu.VMEM(vis.shape, vis.dtype),
             pltpu.VMEM(rows.shape, rows.dtype),
             pltpu.VMEM(cols.shape, cols.dtype),
             pltpu.VMEM(kern.shape, kern.dtype),
-            pltpu.VMEM((2, count + 1, share, wide), jnp.float32),
+            pltpu.VMEM((count + 1, share, wide), jnp.float32),
+            pltpu.VMEM((count + 1, share, wide), jnp.float32),
             pltpu.VMEM((2, 2, count, share, wide // 2), half),
             pltpu.VMEM((2, 2, count, share, wide // 2), half),
             pltpu.VMEM((planes, tiles, share, wide), half),
             pltpu.VMEM((planes, tiles, share, wide), half),
             pltpu.VMEM((planes + 1, tiles, share, wide), half),
             pltpu.VMEM((max(tiles - split, 1), share, wide), half),
-            dma((6,)),
+            dma((5,)),
             dma((2, PIECES)),
             dma,
             dma,

time: 49.2 us -> 48.8 us (level)
  no operation moved by 1% of the time
where the time goes in v5:
time: 48.8 us; the launch traced here: 48.3 us
  Pallas kernels  47.3 us (97%)
  local copies, waits for them, and re-layouts  0.97 us (2%)
    pallas_call x1, Pallas kernels, exchange(): pl.pallas_call(functools.partial(exchange_kernel, planes, tiles), out_sha...  47.3 us

profile of v5, /device:TPU:0, one launch (start us, length us, event | category | flops | bytes accessed | tf_op | source)
XLA Modules:
  0.0 48.3 jit_solution(8516497079913860409)
XLA Ops:
  0.0 47.3 %exchange.1 = f32[32,16,512]{2,1,0:T(8,128)S(1)} custom-call(s32[1,32]{1,0:T(1,128)} %bitcast.11, s32[1,32]{1,0:T(1,128)} %spots.1, bf16[32,2,128]{2,1,0:T(2,128)(2,1)} %bitcast.10, bf16[32,2,2,32,128]{4,3,2,1,0:T(8,128)(2,1)} %bitcast.8, bf16[32,128,256]{2,1,0:T(8,128)(2,1)} %bitcast.7, bf16[512,512]{1,0:T(8,128)(2,1)} %bitcast.9), custom_call_target="tpu_custom_call" | custom-call | tf_op jit(solution)/shard_map/exchange/pallas_call | solution.py:449
  47.3 1.0 %copy.8 = f32[1,32,16,512]{3,2,1,0:T(8,128)} copy(f32[1,32,16,512]{3,2,1,0:T(8,128)S(1)} %bitcast.6) | data formatting | bytes 2097152
